TPU v7x, 128 devices: a whole 4x4x4 slice. The times are simulated.
128 devices in a mesh: front: 4 (over z), grid: 32 (over x, y, core).
Axes of the slice: x: 4, y: 4, z: 4, core: 2. Of those that a mesh axis runs over, the one named last changes fastest.
Arguments:
- child_fronts: float32 [4, 6144, 6144], P('front', 'grid'), as said below
- parent_fronts: float32 [4, 6144, 6144], P('front', 'grid'), as said below
- child_maps: int32 [4, 6144], replicated, may hold values from 0 to 6143, as said below
- parent_of: int32 [4], replicated, may hold values from 0 to 3
- child_pivots: int32 [4], replicated, may hold values from 64 to 256, as said below
- parent_pivots: int32 [4], replicated, may hold values from 64 to 256, as said below
Outputs:
- child_panels: float32 [4, 6144, 256], P('front', 'grid')
- parent_panels: float32 [4, 6144, 256], P('front', 'grid')
- parent_schur: float32 [4, 6144, 6144], P('front', 'grid')
Inputs may be any that keep to these rules, and one draw needn't show every extreme that they name: Each row of child_maps is a permutation: row i of lower front c becomes row child_maps[c, i] of its parent. For i from child_pivots[c] on, child_maps[c, i] strictly increases with i; the rows below child_pivots[c] take the remaining parent indices in increasing order. `parent_of`: entry c names the upper front that receives the contribution block of lower front c. Lower front c eliminates its first child_pivots[c] variables; in every draw some front has exactly 256. Upper front q eliminates its first parent_pivots[q] variables; in every draw some front has exactly 256. `child_fronts`: every front is symmetric positive definite. `parent_fronts`: every front is symmetric positive definite.
All inputs are finite; a program needn't handle non-finite values.
Results may differ from a plain program's by a relative error of at most 0.00011.
Values sent between devices are 32-bit elements; how exact they have to be, the bound alone decides.
A program may use at most 128 MiB of HBM per device.

v0:
```python
import jax
import jax.numpy as jnp
from jax import lax
from jax.sharding import PartitionSpec as P

PMAX = 256


def inverse_factor(pivot_block):
    factor_low = jnp.linalg.cholesky(pivot_block)
    identity = jnp.eye(pivot_block.shape[0], dtype=jnp.float32)
    inverse_low = jax.scipy.linalg.solve_triangular(factor_low, identity, lower=True)
    return inverse_low.T


def factor(front_rows, pivots, first_row):
    local_rows = front_rows.shape[0]
    front_order = front_rows.shape[1]
    position = jnp.arange(PMAX, dtype=jnp.int32)
    pivot_mask = (position < pivots).astype(jnp.float32)
    columns = front_rows[:, :PMAX] * pivot_mask[None, :]
    gathered = lax.all_gather(columns, "grid", axis=0, tiled=True)
    pivot_block = gathered[:PMAX] * pivot_mask[:, None] + jnp.diag(1.0 - pivot_mask)
    inverse_upper = inverse_factor(pivot_block)
    whole_panel = jnp.dot(
        gathered, inverse_upper, precision=lax.Precision.HIGHEST, preferred_element_type=jnp.float32
    )
    panel_rows = lax.dynamic_slice_in_dim(whole_panel, first_row, local_rows, 0)
    schur_rows = front_rows - lax.dot_general(
        panel_rows,
        whole_panel,
        (((1,), (1,)), ((), ())),
        precision=lax.Precision.HIGHEST,
        preferred_element_type=jnp.float32,
    )
    row_mask = (first_row + jnp.arange(local_rows, dtype=jnp.int32) >= pivots).astype(jnp.float32)
    column_mask = (jnp.arange(front_order, dtype=jnp.int32) >= pivots).astype(jnp.float32)
    schur_rows = schur_rows * row_mask[:, None] * column_mask[None, :]
    return (panel_rows, schur_rows)


def on_device(child_fronts, parent_fronts, child_maps, parent_of, child_pivots, parent_pivots):
    front_group = lax.axis_index("front")
    grid_rank = lax.axis_index("grid")
    local_rows = child_fronts.shape[1]
    first_row = grid_rank * local_rows
    fronts = child_maps.shape[0]
    panel_rows, schur_rows = factor(child_fronts[0], child_pivots[front_group], first_row)
    inverse = jnp.argsort(child_maps[front_group])
    mapped = jnp.take(schur_rows, inverse, axis=1)
    targets = (jnp.arange(fronts, dtype=jnp.int32) == parent_of[front_group]).astype(jnp.float32)
    swapped = lax.all_to_all(mapped, "grid", split_axis=1, concat_axis=0, tiled=True)
    turned = jnp.take(swapped.T, inverse, axis=1)
    buffer = targets[:, None, None] * turned[None]
    arrivals = lax.psum_scatter(buffer, "front", scatter_dimension=0, tiled=True)[0]
    assembled = parent_fronts[0] + arrivals
    upper_panel, upper_schur = factor(assembled, parent_pivots[front_group], first_row)
    return (panel_rows[None], upper_panel[None], upper_schur[None])


def solution(mesh):
    in_specs = (P("front", "grid", None), P("front", "grid", None), P(), P(), P(), P())
    out_specs = (P("front", "grid", None), P("front", "grid", None), P("front", "grid", None))
    return jax.shard_map(
        on_device, mesh=mesh, in_specs=in_specs, out_specs=out_specs, check_vma=False
    )
```

profile of v0, /device:TPU:0, one launch (start us, length us, event | category | flops | bytes accessed | tf_op | source)
XLA Modules:
  0.0 638.0 jit_solution(9983429472367905023)
XLA Ops:
  7.2 1.2 dynamic_slice.18
  9.1 1.6 slice_multiply_fusion.1
  10.8 6.7 %sort.17 = (s32[6144]{0:T(1024)}, s32[6144]{0:T(1024)S(1)}) sort(s32[6144]{0:T(1024)S(1)} %bitcast.96, s32[6144]{0:T(1024)S(1)} %iota.127), dimensions={0}, to_apply=%region_4.7 | sort | flops 79872 | bytes 98304 | tf_op jit(solution)/shard_map/jit(argsort)/sort | solution.py:49
  18.2 0.7 compare_convert_fusion.2
  18.9 0.7 fusion.32
  19.6 42.6 %all-gather.3.cloned.1.call-done = f32[6144,256]{1,0:T(8,128)} async-done(((f32[192,256]{1,0:T(8,128)}), f32[6144,256]{1,0:T(8,128)}) %all-gather.3.cloned.1.call-update) | async-done | bytes 6291472 | tf_op jit(solution)/shard_map/all_gather | solution.py:22
  62.3 1.0 slice.67
  63.6 11.7 %cholesky.130 = f32[128,128]{1,0:T(8,128)S(1)} custom-call(f32[128,128]{1,0:T(8,128)S(1)} %cholesky.194), custom_call_target="Cholesky" | custom-call | tf_op jit(solution)/shard_map/jit(cholesky)/cholesky | solution.py:10
  75.4 9.8 %custom-call.13 = f32[1,128,128]{1,2,0:T(8,128)S(1)} custom-call(f32[1,128,128]{2,1,0:T(8,128)S(1)} %get-tuple-element.54), custom_call_target="InvertDiagBlocksLowerTriangular" | custom-call | tf_op jit(solution)/shard_map/jit(cholesky)/cholesky | solution.py:10
  85.7 11.9 %cholesky.147 = f32[128,128]{1,0:T(8,128)S(1)} custom-call(f32[128,128]{1,0:T(8,128)S(1)} %convolution_subtract_fusion.5), custom_call_target="Cholesky" | custom-call | tf_op jit(solution)/shard_map/jit(cholesky)/cholesky | solution.py:10
  99.7 4.0 while.4
  100.3 1.4 bitcast_dynamic-update-slice_fusion.4
  102.3 1.4 bitcast_dynamic-update-slice_fusion.4
  103.7 19.7 %custom-call.14 = f32[2,128,128]{1,2,0:T(8,128)S(1)} custom-call(f32[2,128,128]{2,1,0:T(8,128)S(1)} %get-tuple-element.22), custom_call_target="InvertDiagBlocksLowerTriangular" | custom-call | tf_op jit(solution)/shard_map/jit(_solve_triangular)/triangular_solve | solution.py:12
  124.5 7.7 %fusion.5 = f32[6144,256]{1,0:T(8,128)S(1)} fusion(f32[6144,256]{1,0:T(8,128)} %all-gather.3.cloned.1.call-done, f32[128,256]{1,0:T(8,128)S(1)} %fusion.27, f32[128,256]{1,0:T(8,128)S(1)} %fusion.20), kind=kOutput, calls=%fused_computation.23 | convolution fusion | flops 4831903744 | bytes 12845056 | tf_op jit(solution)/shard_map/dot_general | solution.py:25
  132.2 2.6 copy-done.2
  134.8 8.4 %fusion.3 = f32[192,6144]{1,0:T(8,128)} fusion(f32[6144,256]{1,0:T(8,128)S(1)} %fusion.5, f32[6144]{0:T(1024)S(1)} %fusion.32, f32[192]{0:T(256)S(1)} %compare_convert_fusion.2, s32[]{:T(128)S(6)} %select_n.30, f32[1,192,6144]{2,1,0:T(8,128)S(1)} %bitcast.95), kind=kOutput, calls=%fused_computation.12 | convolution fusion | flops 3627417600 | bytes 15950852 | tf_op jit(solution)/shard_map/dot_general | solution.py:29
  143.2 6.2 copy.19
  149.4 26.6 %gather_fusion = f32[6144,192]{1,0:T(8,128)} fusion(f32[192,6144]{0,1:T(8,128)} %copy.19, s32[6144]{0:T(1024)S(1)} %fusion.34), kind=kCustom, calls=%fused_computation.clone | custom fusion | bytes 9461760 | tf_op jit(solution)/shard_map/jit(_take)/gather | solution.py:50
  176.0 6.8 %broadcast_select_fusion = f32[6144,192]{1,0:T(8,128)} fusion(f32[6144,192]{1,0:T(8,128)} %gather_fusion, pred[6144]{0:T(1024)(128)(4,1)S(1)} %compare_and_fusion), kind=kLoop, calls=%fused_computation.16 | loop fusion | flops 1179648 | bytes 9443328 | tf_op jit(solution)/shard_map/jit(_take)/select_n | solution.py:50
  182.8 5.0 all-to-all-start
  187.8 10.0 %reduce-scatter.2.cloned.1.call-start = ((), (), s32[]{:S(2)}) async-start(), calls=%async_computation.3 | async-start | bytes 23592960 | tf_op jit(solution)/shard_map/reduce_scatter | solution.py:55
  199.1 68.6 %all-to-all-done = f32[192,32,192]{0,2,1:T(8,128)} async-done(((f32[192,32,192]{0,2,1:T(8,128)}), f32[192,32,192]{0,2,1:T(8,128)}, u32[]{:S(2)}, u32[]{:S(2)}) %all-to-all-start) | async-done | bytes 4718624 | tf_op jit(solution)/shard_map/all_to_all | solution.py:52
  267.7 6.9 %copy.20 = f32[32,192,192]{2,1,0:T(8,128)} copy(f32[32,192,192]{1,2,0:T(8,128)} %bitcast.12) | data formatting | bytes 9437184 | tf_op jit(solution)/shard_map/all_to_all | solution.py:52
  274.5 26.5 %gather_fusion.1 = f32[6144,192]{1,0:T(8,128)} fusion(f32[192,6144]{0,1:T(8,128)} %bitcast.89, s32[6144]{0:T(1024)S(1)} %fusion.34), kind=kCustom, calls=%fused_computation.1.clone | custom fusion | bytes 9461760 | tf_op jit(solution)/shard_map/jit(_take)/gather | solution.py:53
  301.0 6.8 %select_bitcast_fusion = f32[192,6144]{0,1:T(8,128)} fusion(f32[6144,192]{1,0:T(8,128)} %gather_fusion.1, pred[6144]{0:T(1024)(128)(4,1)S(1)} %compare_and_fusion), kind=kLoop, calls=%fused_computation.14 | loop fusion | flops 1179648 | bytes 9443328 | tf_op jit(solution)/shard_map/jit(_take)/select_n | solution.py:53
  307.8 6.1 copy.21
  313.9 11.2 %broadcast_multiply_fusion = f32[4,192,6144]{2,1,0:T(8,128)} fusion(f32[192,6144]{1,0:T(8,128)} %copy.21, f32[4]{0:T(128)S(1)} %compare_convert_fusion.3), kind=kLoop, calls=%fused_computation.6 | loop fusion | flops 4718592 | bytes 23592976 | tf_op jit(solution)/shard_map/mul | solution.py:54
  327.0 168.8 %reduce-scatter.2.cloned.1.call-done = f32[1,192,6144]{2,1,0:T(8,128)} async-done(((f32[4,192,6144]{2,1,0:T(8,128)}), f32[1,192,6144]{2,1,0:T(8,128)}) %reduce-scatter.2.cloned.1.call-update) | async-done | bytes 4718608 | tf_op jit(solution)/shard_map/reduce_scatter | solution.py:55
  495.8 4.3 add_bitcast_fusion
  500.1 2.2 copy-done.3
  502.3 0.7 slice_multiply_fusion
  503.0 0.7 broadcast_subtract_fusion
  504.3 0.7 fusion.33
  505.0 1.6 dynamic-slice_bitcast_fusion.1
  506.6 45.0 %all-gather.5.cloned.1.call-done = f32[6144,256]{1,0:T(8,128)} async-done(((f32[192,256]{1,0:T(8,128)}), f32[6144,256]{1,0:T(8,128)}) %all-gather.5.cloned.1.call-update) | async-done | bytes 6291472 | tf_op jit(solution)/shard_map/all_gather | solution.py:22
  551.6 1.0 slice.69
  552.9 11.7 %cholesky.164 = f32[128,128]{1,0:T(8,128)S(1)} custom-call(f32[128,128]{1,0:T(8,128)S(1)} %cholesky.197), custom_call_target="Cholesky" | custom-call | tf_op jit(solution)/shard_map/jit(cholesky)/cholesky | solution.py:10
  564.7 9.8 %custom-call.15 = f32[1,128,128]{1,2,0:T(8,128)S(1)} custom-call(f32[1,128,128]{2,1,0:T(8,128)S(1)} %get-tuple-element.50), custom_call_target="InvertDiagBlocksLowerTriangular" | custom-call | tf_op jit(solution)/shard_map/jit(cholesky)/cholesky | solution.py:10
  575.0 11.7 %cholesky.181 = f32[128,128]{1,0:T(8,128)S(1)} custom-call(f32[128,128]{1,0:T(8,128)S(1)} %convolution_subtract_fusion.4), custom_call_target="Cholesky" | custom-call | tf_op jit(solution)/shard_map/jit(cholesky)/cholesky | solution.py:10
  587.4 0.7 compare_reduce_fusion
  589.4 4.2 while.5
  590.2 1.4 bitcast_dynamic-update-slice_fusion.5
  592.2 1.4 bitcast_dynamic-update-slice_fusion.5
  593.6 19.7 %custom-call.16 = f32[2,128,128]{1,2,0:T(8,128)S(1)} custom-call(f32[2,128,128]{2,1,0:T(8,128)S(1)} %get-tuple-element.23), custom_call_target="InvertDiagBlocksLowerTriangular" | custom-call | tf_op jit(solution)/shard_map/jit(_solve_triangular)/triangular_solve | solution.py:12
  614.4 7.7 %fusion.9 = f32[6144,256]{1,0:T(8,128)S(1)} fusion(f32[6144,256]{1,0:T(8,128)} %all-gather.5.cloned.1.call-done, f32[128,256]{1,0:T(8,128)S(1)} %fusion.23, f32[128,256]{1,0:T(8,128)S(1)} %fusion.18), kind=kOutput, calls=%fused_computation.27 | convolution fusion | flops 4831903744 | bytes 12845056 | tf_op jit(solution)/shard_map/dot_general | solution.py:25
  622.1 0.7 dynamic-slice_bitcast_fusion
  622.8 8.4 %fusion.4 = f32[1,192,6144]{2,1,0:T(8,128)} fusion(f32[192,6144]{1,0:T(8,128)S(1)} %bitcast.92, f32[6144,256]{1,0:T(8,128)S(1)} %fusion.9, f32[6144]{0:T(1024)S(1)} %fusion.33, f32[192]{0:T(256)S(1)} %compare_convert_fusion, s32[]{:T(128)S(6)} %select_n.30), kind=kOutput, calls=%fused_computation.13 | convolution fusion | flops 3627417600 | bytes 15950852 | tf_op jit(solution)/shard_map/dot_general | solution.py:29
  (79 shorter events, 12.9 us)
Async XLA Ops:
  7.2 3.6 copy-start
  7.2 55.1 %all-gather.3.cloned.1.call-start = ((), (), s32[]{:S(2)}) async-start(), calls=%async_computation.2 | async-start | bytes 6488064 | tf_op jit(solution)/shard_map/all_gather | solution.py:22
  124.1 10.7 %slice-start.2 = ((s8[4718592]{0:T(1024)(128)(4,1)}), s8[4194304]{0:T(1024)(128)(4,1)S(1)}, s32[]{:S(2)}) async-start(s8[4718592]{0:T(1024)(128)(4,1)} %bitcast.94), calls=%async_computation.7 | async-start | bytes 8388608
  124.5 10.3 %slice-start.3 = ((s8[4718592]{0:T(1024)(128)(4,1)}), s8[524288]{0:T(1024)(128)(4,1)S(1)}, s32[]{:S(2)}) async-start(s8[4718592]{0:T(1024)(128)(4,1)} %bitcast.94), calls=%async_computation.8 | async-start | bytes 1048576
  132.2 2.6 copy-start.2
  182.8 15.1 %copy-start.4 = (s32[4]{0:T(128)S(1)}, s32[4]{0:T(128)}, u32[]{:S(2)}) copy-start(s32[4]{0:T(128)} %param.14) | copy-start | bytes 52
  182.8 84.9 %all-to-all-start = ((f32[192,32,192]{0,2,1:T(8,128)}), f32[192,32,192]{0,2,1:T(8,128)}, u32[]{:S(2)}, u32[]{:S(2)}) async-start(f32[192,32,192]{0,2,1:T(8,128)} %bitcast.90), calls=%async_computation | async-start | bytes 12582912 | tf_op jit(solution)/shard_map/all_to_all | solution.py:52
  187.8 308.1 %reduce-scatter.2.cloned.1.call-start = ((), (), s32[]{:S(2)}) async-start(), calls=%async_computation.3 | async-start | bytes 23592960 | tf_op jit(solution)/shard_map/reduce_scatter | solution.py:55
  325.1 0.7 copy-start.5
  325.1 226.4 %all-gather.5.cloned.1.call-start = ((), (), s32[]{:S(2)}) async-start(), calls=%async_computation.4 | async-start | bytes 6488064 | tf_op jit(solution)/shard_map/all_gather | solution.py:22
  500.1 2.2 copy-start.3
  614.0 8.8 %slice-start = ((s8[4718592]{0:T(1024)(128)(4,1)}), s8[4194304]{0:T(1024)(128)(4,1)S(1)}, s32[]{:S(2)}) async-start(s8[4718592]{0:T(1024)(128)(4,1)} %bitcast.91), calls=%async_computation.5 | async-start | bytes 8388608
  614.3 8.5 %slice-start.1 = ((s8[4718592]{0:T(1024)(128)(4,1)}), s8[524288]{0:T(1024)(128)(4,1)S(1)}, s32[]{:S(2)}) async-start(s8[4718592]{0:T(1024)(128)(4,1)} %bitcast.91), calls=%async_computation.6 | async-start | bytes 1048576
  622.1 9.1 %copy-start.1 = (s32[4,6144]{1,0:T(4,128)S(1)}, s32[4,6144]{1,0:T(4,128)}, u32[]{:S(2)}) copy-start(s32[4,6144]{1,0:T(4,128)} %param.13) | copy-start | bytes 294916
Sparse Core Ops, SparseCore 0:
  10.9 51.3 all-gather.2
  325.3 170.5 reduce-scatter.1
  503.1 48.3 all-gather.4
where the time goes:
time: 649 us; the launch traced here: 638 us
  waiting for transfers between devices  325 us (50%)
  other arithmetic  152 us (23%)
  local copies, waits for them, and re-layouts  92.9 us (14%)
  matrix products  35.2 us (5%)
  between operations  17 us (3%)
  starting transfers between devices  15.1 us (2%)
    reduce_scatter x1, waiting for transfers between devices, on_device(): lax.psum_scatter(buffer, 'front', scatter_dimension=0, tiled=True)[0]  169 us
    all_gather x2, waiting for transfers between devices, factor(): gathered = lax.all_gather(columns, 'grid', axis=0, tiled=True)  87.6 us
    another operation x13, other arithmetic, inverse_factor(): factor_low = jnp.linalg.cholesky(pivot_block)  68.8 us
    all_to_all x1, waiting for transfers between devices, on_device(): lax.all_to_all(mapped, 'grid', split_axis=1, concat_axis=0, tiled=True)  68.6 us
    another operation x5, other arithmetic, inverse_factor(): jax.scipy.linalg.solve_triangular(factor_low, identity, lower=True)  39.4 us
    gather x1, local copies, waits for them, and re-layouts, on_device(): mapped = jnp.take(schur_rows, inverse, axis=1)  26.6 us
    gather x1, local copies, waits for them, and re-layouts, on_device(): turned = jnp.take(swapped.T, inverse, axis=1)  26.5 us
    dot_general x2, matrix products, factor(): lax.dot_general(panel_rows, whole_panel, (((1,), (1,)), ((), ())), precis...  16.8 us
  transfers between devices with their start and end apart: 4, of which 4 were waited for; matrix products, arithmetic and copies ran while one was open for 2% of the time, Pallas kernels for 0%

commit v1 on v0

v1 whole, which is shorter than its diff:
```python
import functools

import jax
import jax.numpy as jnp
from jax import lax
from jax.experimental import pallas as pl
from jax.experimental.pallas import tpu as pltpu
from jax.sharding import PartitionSpec as P

PMAX = 256
CHIPS = 16
SIDE = 4
ROWS = 192
WIDE = 384
ORDER = 6144
BASE = 32
F32 = jnp.float32
BF16 = jnp.bfloat16
VMEM = pltpu.VMEM
NT = (((1,), (1,)), ((), ()))
NN = (((1,), (0,)), ((), ()))
TN = (((0,), (0,)), ((), ()))


def dot(a, b, dims):
    return lax.dot_general(a, b, dims, preferred_element_type=F32)


def split(a):
    high = a.astype(BF16)
    low = (a - high.astype(F32)).astype(BF16)
    return high, low


def product(a, b, dims):
    a_high, a_low = split(a)
    b_high, b_low = split(b)
    return dot(a_high, b_high, dims) + (dot(a_high, b_low, dims) + dot(a_low, b_high, dims))


def pick(one_hot, a, dims):
    a_high, a_low = split(a)
    return dot(one_hot, a_high, dims) + dot(one_hot, a_low, dims)


def cholesky_kernel(block_ref, inverse_ref, work):
    rows = lax.broadcasted_iota(jnp.int32, (PMAX, PMAX), 0)
    columns = lax.broadcasted_iota(jnp.int32, (PMAX, PMAX), 1)
    work[:, :PMAX] = block_ref[...]
    work[:, PMAX:] = (rows == columns).astype(F32)
    small_rows = lax.broadcasted_iota(jnp.int32, (BASE, 1), 0)
    eye_rows = lax.broadcasted_iota(jnp.int32, (BASE, BASE), 0)
    eye_columns = lax.broadcasted_iota(jnp.int32, (BASE, BASE), 1)
    eye = (eye_rows == eye_columns).astype(F32)
    for step in range(PMAX // BASE):
        first = step * BASE
        last = first + BASE
        diagonal = work[first:last, first:last]
        both = jnp.concatenate([diagonal, eye, jnp.zeros((BASE, 128 - 2 * BASE), F32)], axis=1)
        for k in range(BASE - 1):
            column = both[:, k : k + 1]
            row = both[k : k + 1, :]
            factor = jnp.where(small_rows > k, column / row[:, k : k + 1], 0.0)
            both = both - factor * row
        pivots = jnp.sum(both[:, :BASE] * eye, axis=1, keepdims=True)
        inverse = both[:, BASE : 2 * BASE] / jnp.sqrt(pivots)
        strip = lax.dot_general(
            inverse, work[first:last, :], NN, precision=lax.Precision.HIGHEST, preferred_element_type=F32
        )
        work[first:last, :] = strip
        if last < PMAX:
            update = lax.dot_general(
                strip[:, :PMAX], strip, TN, precision=lax.Precision.HIGHEST, preferred_element_type=F32
            )
            work[last:, :] = work[last:, :] - update[last:, :]
    inverse_ref[...] = work[:, PMAX:]


def inverse_factor(pivot_block):
    return pl.pallas_call(
        cholesky_kernel,
        out_shape=jax.ShapeDtypeStruct((PMAX, PMAX), F32),
        in_specs=[pl.BlockSpec(memory_space=VMEM)],
        out_specs=pl.BlockSpec(memory_space=VMEM),
        scratch_shapes=[pltpu.VMEM((PMAX, 2 * PMAX), F32)],
        cost_estimate=pl.CostEstimate(flops=200_000_000, bytes_accessed=524288, transcendentals=0),
        name="inverse_factor",
    )(pivot_block)


def turn_kernel(map_here, map_next, even_here, even_next, odd_here, odd_next, out_ref, window, places):
    core = lax.axis_index("grid") % 2
    block = pl.program_id(0)
    window[:ROWS, :WIDE] = even_here[...]
    window[:ROWS, WIDE:] = even_next[...]
    window[ROWS:, :WIDE] = odd_here[...]
    window[ROWS:, WIDE:] = odd_next[...]
    places[:, :WIDE] = map_here[...]
    places[:, WIDE:] = map_next[...]
    lanes = pl.ds(pl.multiple_of(core * 128, 128), 512)
    first = block * WIDE + core * ROWS
    wanted = first + lax.broadcasted_iota(jnp.int32, (ROWS, 512), 0)
    one_hot = (wanted == places[:1, lanes]).astype(F32).astype(BF16)
    out_ref[0] = pick(one_hot, window[:, lanes], NT)


def turn(even, odd, places):
    here = lambda rows: pl.BlockSpec((rows, WIDE), lambda j: (0, j))
    after = lambda rows: pl.BlockSpec((rows, WIDE), lambda j: (0, jnp.minimum(j + 1, CHIPS - 1)))
    after_map = pl.BlockSpec((8, WIDE), lambda j: (0, j + 1))
    return pl.pallas_call(
        turn_kernel,
        grid=(CHIPS,),
        out_shape=jax.ShapeDtypeStruct((CHIPS, ROWS, WIDE), F32),
        in_specs=[here(8), after_map, here(ROWS), after(ROWS), here(ROWS), after(ROWS)],
        out_specs=pl.BlockSpec((1, ROWS, WIDE), lambda j: (j, 0, 0)),
        scratch_shapes=[pltpu.VMEM((WIDE, 2 * WIDE), F32), pltpu.VMEM((8, 2 * WIDE), jnp.int32)],
        cost_estimate=pl.CostEstimate(flops=4_000_000_000, bytes_accessed=15_000_000, transcendentals=0),
        name="turn",
    )(places, places, even, even, odd, odd)


def child_kernel(
    map_own, map_before, map_here, own_ref, window_ref, all_ref, inverse_ref, moved_ref,
    panel_ref, schur_ref, strip, places, panel_rows,
):
    step = pl.program_id(0)
    grid_rank = lax.axis_index("grid")
    inverse = inverse_ref[...]

    @pl.when(step == 0)
    def _():
        panel_ref[...] = product(own_ref[...], inverse, NT)
        wanted = grid_rank * ROWS + lax.broadcasted_iota(jnp.int32, (ROWS, 512), 0)
        one_hot = (wanted == map_own[:1, :]).astype(F32).astype(BF16)
        panel_rows[...] = product(pick(one_hot, window_ref[...], NN), inverse, NT)

    strip[:, :WIDE] = strip[:, WIDE:]

    @pl.when(step < CHIPS)
    def _():
        panel = product(all_ref[...], inverse, NT)
        strip[:, WIDE:] = moved_ref[0] - product(panel_rows[...], panel, NT)

    @pl.when(step == CHIPS)
    def _():
        strip[:, WIDE:] = jnp.zeros((ROWS, WIDE), F32)

    @pl.when(step > 0)
    def _():
        places[:, :WIDE] = map_before[...]
        places[:, WIDE:] = map_here[...]
        wanted = (step - 1) * WIDE + lax.broadcasted_iota(jnp.int32, (WIDE, 640), 0)
        one_hot = (wanted == places[:1, :640]).astype(F32).astype(BF16)
        high, low = split(strip[:, :640])
        schur_ref[0] = dot(high, one_hot, NT) + dot(low, one_hot, NT)


def child_schur(places, own_places, own, window, columns, inverse, moved):
    last = CHIPS - 1
    return pl.pallas_call(
        child_kernel,
        grid=(CHIPS + 1,),
        out_shape=(
            jax.ShapeDtypeStruct((ROWS, PMAX), F32),
            jax.ShapeDtypeStruct((CHIPS, ROWS, WIDE), F32),
        ),
        in_specs=[
            pl.BlockSpec((8, 512), lambda j: (0, 0)),
            pl.BlockSpec((8, WIDE), lambda j: (0, jnp.maximum(j - 1, 0))),
            pl.BlockSpec((8, WIDE), lambda j: (0, j)),
            pl.BlockSpec((ROWS, PMAX), lambda j: (0, 0)),
            pl.BlockSpec((512, PMAX), lambda j: (0, 0)),
            pl.BlockSpec((WIDE, PMAX), lambda j: (jnp.minimum(j, last), 0)),
            pl.BlockSpec((PMAX, PMAX), lambda j: (0, 0)),
            pl.BlockSpec((1, ROWS, WIDE), lambda j: (jnp.minimum(j, last), 0, 0)),
        ],
        out_specs=(
            pl.BlockSpec((ROWS, PMAX), lambda j: (0, 0)),
            pl.BlockSpec((1, ROWS, WIDE), lambda j: (jnp.maximum(j - 1, 0), 0, 0)),
        ),
        scratch_shapes=[
            pltpu.VMEM((ROWS, 2 * WIDE), F32),
            pltpu.VMEM((8, 2 * WIDE), jnp.int32),
            pltpu.VMEM((ROWS, PMAX), F32),
        ],
        cost_estimate=pl.CostEstimate(flops=8_000_000_000, bytes_accessed=20_000_000, transcendentals=0),
        name="child_schur",
    )(own_places, places, places, own, window, columns, inverse, moved)


def parent_kernel(
    pivots_ref, weight_ref, own_ref, all_ref, inverse_ref, children_ref, front_ref, panel_ref, schur_ref, panel_rows
):
    step = pl.program_id(0)
    grid_rank = lax.axis_index("grid")
    inverse = inverse_ref[...]

    @pl.when(step == 0)
    def _():
        panel_rows[...] = product(own_ref[...], inverse, NT)
        panel_ref[...] = panel_rows[...]

    panel = product(all_ref[...], inverse, NT)
    total = front_ref[...] - product(panel_rows[...], panel, NT)
    for child in range(SIDE):
        total = total + weight_ref[child] * children_ref[child, 0]
    pivots = pivots_ref[0]
    rows = grid_rank * ROWS + lax.broadcasted_iota(jnp.int32, (ROWS, WIDE), 0)
    columns = step * WIDE + lax.broadcasted_iota(jnp.int32, (ROWS, WIDE), 1)
    schur_ref[...] = jnp.where((rows >= pivots) & (columns >= pivots), total, 0.0)


def parent_schur(pivots, weights, own, columns, inverse, children, front):
    smem = pl.BlockSpec(memory_space=pltpu.SMEM)
    return pl.pallas_call(
        parent_kernel,
        grid=(CHIPS,),
        out_shape=(jax.ShapeDtypeStruct((ROWS, PMAX), F32), jax.ShapeDtypeStruct((ROWS, ORDER), F32)),
        in_specs=[
            smem,
            smem,
            pl.BlockSpec((ROWS, PMAX), lambda j: (0, 0)),
            pl.BlockSpec((WIDE, PMAX), lambda j: (j, 0)),
            pl.BlockSpec((PMAX, PMAX), lambda j: (0, 0)),
            pl.BlockSpec((SIDE, 1, ROWS, WIDE), lambda j: (0, j, 0, 0)),
            pl.BlockSpec((ROWS, WIDE), lambda j: (0, j)),
        ],
        out_specs=(
            pl.BlockSpec((ROWS, PMAX), lambda j: (0, 0)),
            pl.BlockSpec((ROWS, WIDE), lambda j: (0, j)),
        ),
        scratch_shapes=[pltpu.VMEM((ROWS, PMAX), F32)],
        cost_estimate=pl.CostEstimate(flops=4_000_000_000, bytes_accessed=35_000_000, transcendentals=0),
        name="parent_schur",
    )(pivots, weights, own, columns, inverse, children, front)


def pivot_mask(pivots):
    return (jnp.arange(PMAX, dtype=jnp.int32) < pivots).astype(F32)


def pivot_block(columns, mask):
    return columns[:PMAX] * mask[:, None] + jnp.diag(1.0 - mask)


def on_device(child_fronts, parent_fronts, child_maps, parent_of, child_pivots, parent_pivots):
    front_group = lax.axis_index("front")
    grid_rank = lax.axis_index("grid")
    core = grid_rank % 2
    front_rows = child_fronts[0]
    child_map = child_maps[front_group]
    pivots = child_pivots[front_group]

    sibling = lax.ppermute(front_rows, "grid", [(g, g ^ 1) for g in range(2 * CHIPS)])
    even = jnp.where(core == 0, front_rows, sibling)
    odd = jnp.where(core == 0, sibling, front_rows)
    position = jnp.arange(ORDER, dtype=jnp.int32)
    line = jnp.where(position >= pivots, child_map, -1)
    line = jnp.pad(line, (0, 2 * WIDE), constant_values=-1)
    places = jnp.broadcast_to(line[None], (8, line.shape[0]))
    turned = turn(even, odd, places)
    same_core = [[2 * chip + k for chip in range(CHIPS)] for k in range(2)]
    moved = lax.all_to_all(turned, "grid", 0, 0, axis_index_groups=same_core)

    mask = pivot_mask(pivots)
    own = front_rows[:, :PMAX] * mask[None, :]
    columns = lax.all_gather(own, "grid", axis=0, tiled=True)
    inverse = inverse_factor(pivot_block(columns, mask))
    first = grid_rank * ROWS
    start = jnp.minimum(first, ORDER - 512)
    window = lax.dynamic_slice(columns, (start, 0), (512, PMAX))
    own_places = lax.dynamic_slice(places, (0, start), (8, 512))
    panel_rows, schur = child_schur(places, own_places, own, window, columns, inverse, moved)

    upper_pivots = parent_pivots[front_group]
    upper_mask = pivot_mask(upper_pivots)
    weights = (parent_of == front_group).astype(F32)
    leading = lax.all_gather(schur[0, :, :PMAX], "front", axis=0)
    upper_own = parent_fronts[0, :, :PMAX]
    for child in range(SIDE):
        upper_own = upper_own + weights[child] * leading[child]
    upper_own = upper_own * upper_mask[None, :]
    upper_columns = lax.all_gather(upper_own, "grid", axis=0, tiled=True)
    children = lax.all_gather(schur, "front", axis=0)
    upper_inverse = inverse_factor(pivot_block(upper_columns, upper_mask))
    upper_panel, upper_schur = parent_schur(
        upper_pivots[None], weights, upper_own, upper_columns, upper_inverse, children, parent_fronts[0]
    )
    return (panel_rows[None], upper_panel[None], upper_schur[None])


def solution(mesh):
    in_specs = (P("front", "grid", None), P("front", "grid", None), P(), P(), P(), P())
    out_specs = (P("front", "grid", None), P("front", "grid", None), P("front", "grid", None))
    return jax.shard_map(
        on_device, mesh=mesh, in_specs=in_specs, out_specs=out_specs, check_vma=False
    )
```

time: 649 us -> 436 us (0.67); the launches traced: 638 us -> 434 us
  other arithmetic: 152 us -> 21.2 us
  Pallas kernels: 0 us -> 127 us
  local copies, waits for them, and re-layouts: 92.9 us -> 6.81 us
  waiting for transfers between devices: 325 us -> 244 us
  matrix products: 35.2 us -> 0 us
  blocking collectives: 0 us -> 13.8 us
  starting transfers between devices: 15.1 us -> 7.7 us
    reduce_scatter x1 -> x0, waiting for transfers between devices: 169 us -> none  [on_device(): lax.psum_scatter(buffer, 'front', scatter_dimension=0, tiled=True)[0]]
    pallas_call x0 -> x5, Pallas kernels: none -> 127 us  [the longest x2 58.2 us: inverse_factor(): pl.pallas_call(cholesky_kernel, out_shape=jax.ShapeDtypeStruct((PMAX, PMA...]
    all_gather x2 -> x3, waiting for transfers between devices: 87.6 us -> 211 us  [the longest x1 143 us: on_device(): children = lax.all_gather(schur, 'front', axis=0)]
    another operation x18 -> x0, other arithmetic: 108 us -> none  [the longest x13 68.8 us: inverse_factor(): factor_low = jnp.linalg.cholesky(pivot_block)]
    gather x2 -> x0, local copies, waits for them, and re-layouts: 53.1 us -> none  [the longest x1 26.6 us: on_device(): mapped = jnp.take(schur_rows, inverse, axis=1)]
    all_to_all x1, waiting for transfers between devices: 68.6 us -> 24.4 us  [on_device(): moved = lax.all_to_all(turned, 'grid', 0, 0, axis_index_groups=same_core)]
    dot_general x4 -> x0, matrix products: 32.3 us -> none  [the longest x2 16.8 us: factor(): lax.dot_general(panel_rows, whole_panel, (((1,), (1,)), ((), ())), precis...]
    all_gather x0 -> x1, blocking collectives: none -> 13.8 us  [on_device(): leading = lax.all_gather(schur[0, :, :PMAX], 'front', axis=0)]
  transfers between devices with their start and end apart: 4 -> 5, of which waited for: 4 -> 5; matrix products, arithmetic and copies ran while one was open for 2% -> 4% of each run, Pallas kernels for 0% -> 18%
where the time goes in v1:
time: 436 us; the launch traced here: 434 us
  waiting for transfers between devices  244 us (56%)
  Pallas kernels  127 us (29%)
  other arithmetic  21.2 us (5%)
  between operations  13.9 us (3%)
  blocking collectives  13.8 us (3%)
  starting transfers between devices  7.7 us (2%)
  local copies, waits for them, and re-layouts  6.81 us (2%)
    all_gather x1, waiting for transfers between devices, on_device(): children = lax.all_gather(schur, 'front', axis=0)  143 us
    pallas_call x2, Pallas kernels, inverse_factor(): pl.pallas_call(cholesky_kernel, out_shape=jax.ShapeDtypeStruct((PMAX, PMA...  58.2 us
    all_gather x1, waiting for transfers between devices, on_device(): upper_columns = lax.all_gather(upper_own, 'grid', axis=0, tiled=True)  49.9 us
    pallas_call x1, Pallas kernels, child_schur(): pl.pallas_call(child_kernel, grid=(CHIPS + 1,), out_shape=(jax.ShapeDtype...  27.4 us
    all_to_all x1, waiting for transfers between devices, on_device(): moved = lax.all_to_all(turned, 'grid', 0, 0, axis_index_groups=same_core)  24.4 us
    pallas_call x1, Pallas kernels, parent_schur(): pl.pallas_call(parent_kernel, grid=(CHIPS,), out_shape=(jax.ShapeDtypeStr...  23.5 us
    all_gather x1, waiting for transfers between devices, on_device(): columns = lax.all_gather(own, 'grid', axis=0, tiled=True)  18.3 us
    pallas_call x1, Pallas kernels, turn(): pl.pallas_call(turn_kernel, grid=(CHIPS,), out_shape=jax.ShapeDtypeStruct...  18.1 us
  transfers between devices with their start and end apart: 5, of which 5 were waited for; matrix products, arithmetic and copies ran while one was open for 4% of the time, Pallas kernels for 18%

profile of v1, /device:TPU:0, one launch (start us, length us, event | category | flops | bytes accessed | tf_op | source)
XLA Modules:
  0.0 434.1 jit_solution(2244919280735218586)
XLA Ops:
  7.2 0.0 copy-start
  7.2 0.0 all-gather.5.cloned.1.call-start
  7.2 1.2 dynamic_slice.15
  8.5 0.6 compare_convert_fusion.2
  9.1 1.6 slice_multiply_fusion.6.own_ref
  10.8 0.0 all-gather.5.cloned.1.call-update
  10.8 0.1 collective-permute-start
  10.9 0.0 copy-done
  10.9 0.7 fusion.8
  11.6 7.5 %collective-permute-done = f32[192,6144]{1,0:T(8,128)} collective-permute-done((f32[192,6144]{1,0:T(8,128)}, f32[192,6144]{1,0:T(8,128)}, u32[]{:S(2)}, u32[]{:S(2)}) %collective-permute-start) | collective-permute-done | bytes 4718624 | tf_op jit(solution)/shard_map/ppermute | solution.py:255
  19.1 8.7 %broadcast_select_fusion = (f32[192,6144]{1,0:T(8,128)}, f32[192,6144]{1,0:T(8,128)}) fusion(f32[192,6144]{1,0:T(8,128)} %collective-permute-done, pred[]{:T(512)S(6)} %eq.20, f32[1,192,6144]{2,1,0:T(8,128)} %param.6), kind=kLoop, calls=%fused_computation | loop fusion | flops 2359296 | bytes 18874368 | tf_op jit(solution)/shard_map/jit(_where)/select_n | solution.py:257
  27.8 0.7 broadcast_in_dim.52.map_here.map_next.map_before
  28.5 18.1 %turn.1 = f32[16,192,384]{2,1,0:T(8,128)} custom-call(s32[8,6912]{1,0:T(8,128)} %broadcast_in_dim.52.map_here.map_next.map_before, s32[8,6912]{1,0:T(8,128)} %broadcast_in_dim.52.map_here.map_next.map_before, f32[192,6144]{1,0:T(8,128)} %get-tuple-element.12.even_here.even_next, f32[192,6144]{1,0:T(8,128)} %get-tuple-element.12.even_here.even_next, ...), custom_call_target="tpu_custom_call" | custom-call | flops 4000000000 | bytes 15000000 | tf_op jit(solution)/shard_map/turn/pallas_call | solution.py:111
  46.7 0.0 copy-start.3
  46.7 0.0 copy-start.4
  46.7 7.3 %all-to-all-start = ((f32[16,192,384]{2,1,0:T(8,128)}), f32[16,192,384]{2,1,0:T(8,128)}, u32[]{:S(2)}, u32[]{:S(2)}) async-start(f32[16,192,384]{2,1,0:T(8,128)} %turn.1), calls=%async_computation | async-start | bytes 9437184 | tf_op jit(solution)/shard_map/all_to_all | solution.py:264
  54.0 0.0 all-gather.7.cloned.1.call-start
  54.0 0.0 copy-done.3
  54.0 0.6 dynamic_slice.19.pivots_ref
  54.7 0.6 broadcast_subtract_fusion.1
  55.3 0.6 compare_convert_fusion
  56.0 0.1 pad_dynamic-slice_fusion
  56.1 0.0 copy-done.4
  56.1 0.0 copy-start.2
  56.1 0.7 fusion.9
  56.7 18.3 %all-gather.5.cloned.1.call-done.all_ref = f32[6144,256]{1,0:T(8,128)} async-done(((f32[192,256]{1,0:T(8,128)}), f32[6144,256]{1,0:T(8,128)}) %all-gather.5.cloned.1.call-update) | async-done | bytes 6291472 | tf_op jit(solution)/shard_map/all_gather | solution.py:268
  75.0 1.8 fusion.1.block_ref
  76.8 29.1 %inverse_factor.2.inverse_ref = f32[256,256]{1,0:T(8,128)} custom-call(f32[256,256]{1,0:T(8,128)} %fusion.1.block_ref), custom_call_target="tpu_custom_call" | custom-call | flops 200000000 | bytes 524288 | tf_op jit(solution)/shard_map/inverse_factor/pallas_call | solution.py:80
  105.9 1.9 constant_dynamic-slice_fusion.window_ref
  107.8 24.4 %all-to-all-done.moved_ref = f32[16,192,384]{2,1,0:T(8,128)} async-done(((f32[16,192,384]{2,1,0:T(8,128)}), f32[16,192,384]{2,1,0:T(8,128)}, u32[]{:S(2)}, u32[]{:S(2)}) %all-to-all-start) | async-done | bytes 4718624 | tf_op jit(solution)/shard_map/all_to_all | solution.py:264
  132.1 0.6 broadcast_in_dim.51.map_own
  132.7 27.4 %child_schur.1 = (f32[192,256]{1,0:T(8,128)}, f32[16,192,384]{2,1,0:T(8,128)}) custom-call(s32[8,512]{1,0:T(8,128)} %broadcast_in_dim.51.map_own, s32[8,6912]{1,0:T(8,128)} %broadcast_in_dim.52.map_here.map_next.map_before, s32[8,6912]{1,0:T(8,128)} %broadcast_in_dim.52.map_here.map_next.map_before, f32[192,256]{1,0:T(8,128)} %slice_multiply_fusion.6.own_ref, ...), custom_call_target="tpu_custom_call" | custom-call | flops 8000000000 | bytes 20000000 | tf_op jit(solution)/shard_map/child_schur/pallas_call | solution.py:161
  160.1 0.0 copy-done.2
  160.1 0.9 slice.43
  161.0 13.8 %all_gather.16 = f32[4,192,256]{2,1,0:T(8,128)S(1)} all-gather(f32[1,192,256]{2,1,0:T(8,128)S(1)} %slice.43), channel_id=1, replica_groups=mesh['front'=4,'grid'=32] {'front'}, dimensions={0}, use_global_device_ids=true | all-gather | bytes 983040 | tf_op jit(solution)/shard_map/all_gather | solution.py:279
  174.8 4.1 fusion.4.own_ref
  178.9 0.0 all-gather.7.cloned.1.call-update
  178.9 0.2 all-gather.9.cloned.1.call-start
  179.2 0.5 all-gather.9.cloned.1.call-update
  179.7 0.6 broadcast_subtract_fusion
  180.3 49.9 %all-gather.7.cloned.1.call-done.all_ref = f32[6144,256]{1,0:T(8,128)} async-done(((f32[192,256]{1,0:T(8,128)}), f32[6144,256]{1,0:T(8,128)}) %all-gather.7.cloned.1.call-update) | async-done | bytes 6291472 | tf_op jit(solution)/shard_map/all_gather | solution.py:284
  230.2 1.8 fusion.block_ref
  232.0 29.1 %inverse_factor.3.inverse_ref = f32[256,256]{1,0:T(8,128)} custom-call(f32[256,256]{1,0:T(8,128)} %fusion.block_ref), custom_call_target="tpu_custom_call" | custom-call | flops 200000000 | bytes 524288 | tf_op jit(solution)/shard_map/inverse_factor/pallas_call | solution.py:80
  261.1 142.9 %all-gather.9.cloned.1.call-done = f32[64,192,384]{2,1,0:T(8,128)} async-done(((f32[16,192,384]{2,1,0:T(8,128)}), f32[64,192,384]{2,1,0:T(8,128)}) %all-gather.9.cloned.1.call-update) | async-done | bytes 18874384 | tf_op jit(solution)/shard_map/all_gather | solution.py:285
  404.1 0.0 copy-start.1
  404.1 23.5 %parent_schur.1 = (f32[192,256]{1,0:T(8,128)}, f32[192,6144]{1,0:T(8,128)}) custom-call(s32[1]{0:T(128)} %dynamic_slice.19.pivots_ref, f32[4]{0:T(128)} %copy-done.2, f32[192,256]{1,0:T(8,128)} %fusion.4.own_ref, f32[6144,256]{1,0:T(8,128)} %all-gather.7.cloned.1.call-done.all_ref, f32[256,256]{1,0:T(8,128)} %inverse_factor.3.inverse_ref, ...), custom_call_target="tpu_custom_call" | custom-call | flops 4000000000 | bytes 35000000 | tf_op jit(solution)/shard_map/parent_schur/pallas_call | solution.py:216
  427.5 0.0 copy-done.1
  (3 shorter events, 0.0 us)
Async XLA Ops:
  7.2 3.7 copy-start
  7.2 67.8 %all-gather.5.cloned.1.call-start = ((), (), s32[]{:S(2)}) async-start(), calls=%async_computation.1 | async-start | bytes 6488064 | tf_op jit(solution)/shard_map/all_gather | solution.py:268
  10.8 8.3 %collective-permute-start = (f32[192,6144]{1,0:T(8,128)}, f32[192,6144]{1,0:T(8,128)}, u32[]{:S(2)}, u32[]{:S(2)}) collective-permute-start(f32[192,6144]{1,0:T(8,128)} %bitcast.21), channel_id=1, source_target_pairs={{0,1},{1,0},{2,3},{3,2},{4,5},{5,4},{6,7},{7,6},{8,9},{9,8},{10,11... | collective-permute-start | bytes 14155784 | tf_op jit(solution)/shard_map/ppermute | solution.py:255
  46.7 7.4 %copy-start.3 = (s32[4]{0:T(128)S(1)}, s32[4]{0:T(128)}, u32[]{:S(2)}) copy-start(s32[4]{0:T(128)} %param.11) | copy-start | bytes 52
  46.7 9.4 %copy-start.4 = (s32[4]{0:T(128)S(1)}, s32[4]{0:T(128)}, u32[]{:S(2)}) copy-start(s32[4]{0:T(128)} %param.9) | copy-start | bytes 52
  46.7 85.5 %all-to-all-start = ((f32[16,192,384]{2,1,0:T(8,128)}), f32[16,192,384]{2,1,0:T(8,128)}, u32[]{:S(2)}, u32[]{:S(2)}) async-start(f32[16,192,384]{2,1,0:T(8,128)} %turn.1), calls=%async_computation | async-start | bytes 9437184 | tf_op jit(solution)/shard_map/all_to_all | solution.py:264
  54.0 176.2 %all-gather.7.cloned.1.call-start = ((), (), s32[]{:S(2)}) async-start(), calls=%async_computation.2 | async-start | bytes 6488064 | tf_op jit(solution)/shard_map/all_gather | solution.py:284
  56.1 104.0 %copy-start.2 = (f32[4]{0:T(128)}, f32[4]{0:T(128)S(1)}, u32[]{:S(2)}) copy-start(f32[4]{0:T(128)S(1)} %compare_convert_fusion.1.weight_ref) | copy-start | bytes 52
  178.9 225.1 %all-gather.9.cloned.1.call-start = ((), (), s32[]{:S(2)}) async-start(), calls=%async_computation.3 | async-start | bytes 23592960 | tf_op jit(solution)/shard_map/all_gather | solution.py:285
  404.1 23.5 %copy-start.1 = (s32[4,6144]{1,0:T(4,128)S(1)}, s32[4,6144]{1,0:T(4,128)}, u32[]{:S(2)}) copy-start(s32[4,6144]{1,0:T(4,128)} %param.8) | copy-start | bytes 294916
Sparse Core Ops, SparseCore 0:
  10.9 64.0 all-gather.4
  179.1 51.1 all-gather.6
  232.5 171.5 all-gather.8

commit v2 on v1

v2 whole, which is shorter than its diff:
```python
import functools

import jax
import jax.numpy as jnp
from jax import lax
from jax.experimental import pallas as pl
from jax.experimental.pallas import tpu as pltpu
from jax.sharding import PartitionSpec as P

PMAX = 256
CHIPS = 16
SIDE = 4
ROWS = 192
WIDE = 384
ORDER = 6144
BASE = 32
LEAD = 256
MESH = pl.DeviceIdType.MESH
SELF = ((0, 0), (0, 2), (2, 0), (2, 2))
TURNED = ((0, 1), (1, 0), (3, 3), (3, 1), (1, 2), (2, 3))
F32 = jnp.float32
BF16 = jnp.bfloat16
VMEM = pltpu.VMEM
NT = (((1,), (1,)), ((), ()))
NN = (((1,), (0,)), ((), ()))
TN = (((0,), (0,)), ((), ()))


def dot(a, b, dims):
    return lax.dot_general(a, b, dims, preferred_element_type=F32)


def split(a):
    high = a.astype(BF16)
    low = (a - high.astype(F32)).astype(BF16)
    return high, low


def product(a, b, dims):
    a_high, a_low = split(a)
    b_high, b_low = split(b)
    return dot(a_high, b_high, dims) + (dot(a_high, b_low, dims) + dot(a_low, b_high, dims))


def pick(one_hot, a, dims):
    a_high, a_low = split(a)
    return dot(one_hot, a_high, dims) + dot(one_hot, a_low, dims)


def exact(a, b, dims):
    return lax.dot_general(a, b, dims, precision=lax.Precision.HIGHEST, preferred_element_type=F32)


def shifted(chip, offset, sign=1):
    x = (chip // SIDE + sign * offset[0] + SIDE) % SIDE
    y = (chip % SIDE + sign * offset[1] + SIDE) % SIDE
    return x * SIDE + y


def remote(src, dst, sems, index, device):
    return pltpu.make_async_remote_copy(
        src_ref=src, dst_ref=dst, send_sem=sems[0].at[index], recv_sem=sems[1].at[index],
        device_id=device, device_id_type=MESH,
    )


def greet(devices):
    barrier = pltpu.get_barrier_semaphore()
    for device in devices:
        pl.semaphore_signal(barrier, inc=1, device_id=device, device_id_type=MESH)
    pl.semaphore_wait(barrier, len(devices))


def cholesky_kernel(pivots_ref, block_ref, inverse_ref, work):
    rows = lax.broadcasted_iota(jnp.int32, (PMAX, PMAX), 0)
    columns = lax.broadcasted_iota(jnp.int32, (PMAX, PMAX), 1)
    same = (rows == columns).astype(F32)
    pivots = pivots_ref[0]
    work[:, :PMAX] = jnp.where((rows < pivots) & (columns < pivots), block_ref[...], same)
    work[:, PMAX:] = same
    small_rows = lax.broadcasted_iota(jnp.int32, (BASE, 1), 0)
    eye_rows = lax.broadcasted_iota(jnp.int32, (BASE, BASE), 0)
    eye_columns = lax.broadcasted_iota(jnp.int32, (BASE, BASE), 1)
    eye = (eye_rows == eye_columns).astype(F32)
    for step in range(PMAX // BASE):
        first = step * BASE
        last = first + BASE
        diagonal = work[first:last, first:last]
        both = jnp.concatenate([diagonal, eye, jnp.zeros((BASE, 128 - 2 * BASE), F32)], axis=1)
        for k in range(BASE - 1):
            column = jnp.where(small_rows > k, both[:, k : k + 1], 0.0)
            row = both[k : k + 1, :]
            both = both - column * (row / row[:, k : k + 1])
        pivot_values = jnp.sum(both[:, :BASE] * eye, axis=1, keepdims=True)
        inverse = both[:, BASE : 2 * BASE] / jnp.sqrt(pivot_values)
        strip = exact(inverse, work[first:last, :], NN)
        work[first:last, :] = strip
        if last < PMAX:
            update = exact(strip[:, :PMAX], strip, TN)
            work[last:, :] = work[last:, :] - update[last:, :]
    inverse_ref[...] = work[:, PMAX:]


def inverse_factor(pivots, columns):
    return pl.pallas_call(
        cholesky_kernel,
        grid=(1,),
        out_shape=jax.ShapeDtypeStruct((PMAX, PMAX), F32),
        in_specs=[pl.BlockSpec(memory_space=pltpu.SMEM), pl.BlockSpec((PMAX, PMAX), lambda j: (0, 0))],
        out_specs=pl.BlockSpec((PMAX, PMAX), lambda j: (0, 0)),
        scratch_shapes=[pltpu.VMEM((PMAX, 2 * PMAX), F32)],
        cost_estimate=pl.CostEstimate(flops=400_000_000, bytes_accessed=524288, transcendentals=0),
        name="inverse_factor",
    )(pivots, columns)


def gather_kernel(own_ref, all_ref, local_sem, send_sems, recv_sems):
    rank = lax.axis_index("grid")
    core = rank % 2
    chip = rank // 2
    x, y = chip // SIDE, chip % SIDE
    p = y + core * (x - y)
    s = x + core * (y - x)

    def device(dp, ds):
        pp, ss = (p + dp) % SIDE, (s + ds) % SIDE
        return 2 * (pp * (1 + 3 * core) + ss * (4 - 3 * core)) + core

    def rows(dp, ds, half=None):
        first = device(dp, ds) * ROWS
        if half is None:
            return pl.ds(pl.multiple_of(first, 64), ROWS)
        return pl.ds(pl.multiple_of(first + half * (ROWS // 2), 32), ROWS // 2)

    sems = (send_sems, recv_sems)
    sibling = {"grid": rank + 1 - 2 * core}
    p_up, p_down = {"grid": device(1, 0)}, {"grid": device(3, 0)}
    s_up, s_down = {"grid": device(0, 1)}, {"grid": device(0, 3)}
    greet((p_up, p_down, s_up, s_down, sibling))
    here = pltpu.make_async_copy(own_ref, all_ref.at[rows(0, 0)], local_sem)
    here.start()
    copies = []

    def send(index, where, target, source=None):
        copy = remote(all_ref.at[where] if source is None else source, all_ref.at[where], sems, index, target)
        copy.start()
        copies.append(copy)

    def arrived(index, where):
        remote(all_ref.at[where], all_ref.at[where], sems, index, sibling).wait_recv()

    def across(dp, ds, source=None):
        send(20 + 4 * dp + ds, rows(dp, ds), sibling, source)

    def sideways(dp):
        send(4 + dp, rows(dp, 0), s_up)
        send(8 + dp, rows(dp, 0), s_down)

    send(0, rows(0, 0), p_up, own_ref)
    send(1, rows(0, 0), p_down, own_ref)
    send(4, rows(0, 0), s_up, own_ref)
    send(8, rows(0, 0), s_down, own_ref)
    across(0, 0, own_ref)
    arrived(0, rows(3, 0))
    send(2, rows(3, 0, 0), p_up)
    sideways(3)
    across(3, 0)
    arrived(1, rows(1, 0))
    send(3, rows(1, 0, 1), p_down)
    sideways(1)
    across(1, 0)

    def pass_on(dp):
        arrived(4 + dp, rows(dp, 3))
        send(12 + dp, rows(dp, 3, 0), s_up)
        across(dp, 3)
        arrived(8 + dp, rows(dp, 1))
        send(16 + dp, rows(dp, 1, 1), s_down)
        across(dp, 1)

    pass_on(0)
    arrived(2, rows(2, 0, 0))
    arrived(3, rows(2, 0, 1))
    sideways(2)
    across(2, 0)
    for dp in (3, 1, 2):
        pass_on(dp)
    for dp in (0, 3, 1, 2):
        arrived(12 + dp, rows(dp, 2, 0))
        arrived(16 + dp, rows(dp, 2, 1))
        across(dp, 2)
    for copy in copies:
        copy.wait_send()
    for dp in range(SIDE):
        for ds in range(SIDE):
            chip_there = ((s + dp) % SIDE) * (4 - 3 * core) + ((p + ds) % SIDE) * (1 + 3 * core)
            first = (2 * chip_there + 1 - core) * ROWS
            arrived(20 + 4 * dp + ds, pl.ds(pl.multiple_of(first, 64), ROWS))
    here.wait()


def gather_rows(own, collective_id):
    return pl.pallas_call(
        gather_kernel,
        out_shape=jax.ShapeDtypeStruct((ORDER, PMAX), F32),
        in_specs=[pl.BlockSpec(memory_space=VMEM)],
        out_specs=pl.BlockSpec(memory_space=VMEM),
        scratch_shapes=[
            pltpu.SemaphoreType.DMA,
            pltpu.SemaphoreType.DMA((36,)),
            pltpu.SemaphoreType.DMA((36,)),
        ],
        compiler_params=pltpu.CompilerParams(collective_id=collective_id, has_side_effects=True),
        cost_estimate=pl.CostEstimate(flops=400_000_000, bytes_accessed=6_300_000, transcendentals=0),
        name="gather_rows",
    )(own)


def lead_kernel(pivots_ref, weight_ref, lead_ref, front_ref, out_ref, landing, send_sems, recv_sems):
    group = lax.axis_index("front")
    others = [{"front": (group + d) % SIDE} for d in range(1, SIDE)]
    greet(others)
    sems = (send_sems, recv_sems)
    copies = [remote(lead_ref.at[:, pl.ds(0, LEAD)], landing.at[d], sems, d, others[d]) for d in range(SIDE - 1)]
    for copy in copies:
        copy.start()
    pivots = pivots_ref[0]
    total = front_ref[...] + weight_ref[0] * lead_ref[:, :LEAD]
    for d in range(SIDE - 1):
        copies[d].wait()
        total = total + weight_ref[d + 1] * landing[d]
    columns = lax.broadcasted_iota(jnp.int32, (ROWS, LEAD), 1)
    out_ref[...] = jnp.where(columns < pivots, total, 0.0)


def lead_columns(pivots, weights, lead, front):
    smem = pl.BlockSpec(memory_space=pltpu.SMEM)
    return pl.pallas_call(
        lead_kernel,
        grid=(1,),
        out_shape=jax.ShapeDtypeStruct((ROWS, LEAD), F32),
        in_specs=[
            smem, smem,
            pl.BlockSpec((ROWS, WIDE), lambda j: (0, 0)),
            pl.BlockSpec((ROWS, LEAD), lambda j: (0, 0)),
        ],
        out_specs=pl.BlockSpec((ROWS, LEAD), lambda j: (0, 0)),
        scratch_shapes=[
            pltpu.VMEM((SIDE - 1, ROWS, LEAD), F32),
            pltpu.SemaphoreType.DMA((SIDE - 1,)),
            pltpu.SemaphoreType.DMA((SIDE - 1,)),
        ],
        compiler_params=pltpu.CompilerParams(collective_id=2, has_side_effects=True),
        cost_estimate=pl.CostEstimate(flops=200_000_000, bytes_accessed=1_000_000, transcendentals=0),
        name="lead_columns",
    )(pivots, weights, lead, front)


def fold_kernel(weight_ref, children_ref, sum_ref, mirror_ref):
    total = weight_ref[0] * children_ref[0, 0]
    for child in range(1, SIDE):
        total = total + weight_ref[child] * children_ref[child, 0]
    sum_ref[0] = total
    turned = total.T
    mirror_ref[0, 0] = turned[:ROWS]
    mirror_ref[0, 1] = turned[ROWS:]


def fold(weights, children):
    count = len(TURNED)
    return pl.pallas_call(
        fold_kernel,
        grid=(count,),
        out_shape=(
            jax.ShapeDtypeStruct((count, ROWS, WIDE), F32),
            jax.ShapeDtypeStruct((count, 2, ROWS, ROWS), F32),
        ),
        in_specs=[
            pl.BlockSpec(memory_space=pltpu.SMEM),
            pl.BlockSpec((SIDE, 1, ROWS, WIDE), lambda i: (0, i, 0, 0)),
        ],
        out_specs=(
            pl.BlockSpec((1, ROWS, WIDE), lambda i: (i, 0, 0)),
            pl.BlockSpec((1, 2, ROWS, ROWS), lambda i: (i, 0, 0, 0)),
        ),
        cost_estimate=pl.CostEstimate(flops=100_000_000, bytes_accessed=12_000_000, transcendentals=0),
        name="fold",
    )(weights, children)


def mirror_kernel(mirror_ref, landing_ref, send_sems, recv_sems):
    rank = lax.axis_index("grid")
    core = rank % 2
    chip = rank // 2
    sems = (send_sems, recv_sems)
    targets, sources = [], []
    for offset in TURNED:
        for k in range(2):
            targets.append({"grid": 2 * shifted(chip, offset) + k})
            sources.append({"grid": 2 * shifted(chip, offset, -1) + k})
    barrier = pltpu.get_barrier_semaphore()
    for device in sources:
        pl.semaphore_signal(barrier, inc=1, device_id=device, device_id_type=MESH)
    pl.semaphore_wait(barrier, len(targets))
    count = len(TURNED)
    copies = []
    for i in range(count):
        for k in range(2):
            copy = pltpu.make_async_remote_copy(
                src_ref=mirror_ref.at[i, k],
                dst_ref=landing_ref.at[i, core],
                send_sem=send_sems.at[2 * i + k],
                recv_sem=recv_sems.at[2 * i + core],
                device_id=targets[2 * i + k],
                device_id_type=MESH,
            )
            copy.start()
            copies.append(copy)
    for copy in copies:
        copy.wait_send()
    for i in range(count):
        for k in range(2):
            remote(mirror_ref.at[i, k], landing_ref.at[i, k], sems, 2 * i + k, targets[0]).wait_recv()


def mirror_blocks(mirror):
    count = len(TURNED)
    return pl.pallas_call(
        mirror_kernel,
        out_shape=jax.ShapeDtypeStruct((count, 2, ROWS, ROWS), F32),
        in_specs=[pl.BlockSpec(memory_space=VMEM)],
        out_specs=pl.BlockSpec(memory_space=VMEM),
        scratch_shapes=[pltpu.SemaphoreType.DMA((2 * count,)), pltpu.SemaphoreType.DMA((2 * count,))],
        compiler_params=pltpu.CompilerParams(collective_id=3, has_side_effects=True),
        cost_estimate=pl.CostEstimate(flops=400_000_000, bytes_accessed=5_000_000, transcendentals=0),
        name="mirror_blocks",
    )(mirror)


def turn_kernel(map_here, map_next, own_here, own_next, pair_here, pair_next, out_ref, window, places):
    core = lax.axis_index("grid") % 2
    block = pl.program_id(0)
    own = pl.ds(pl.multiple_of(core * ROWS, 64), ROWS)
    pair = pl.ds(pl.multiple_of((1 - core) * ROWS, 64), ROWS)
    window[own, :WIDE] = own_here[...]
    window[own, WIDE:] = own_next[...]
    window[pair, :WIDE] = pair_here[...]
    window[pair, WIDE:] = pair_next[...]
    places[:, :WIDE] = map_here[...]
    places[:, WIDE:] = map_next[...]
    lanes = pl.ds(pl.multiple_of(core * 128, 128), 512)
    first = block * WIDE + core * ROWS
    wanted = first + lax.broadcasted_iota(jnp.int32, (ROWS, 512), 0)
    one_hot = (wanted == places[:1, lanes]).astype(F32).astype(BF16)
    out_ref[0] = pick(one_hot, window[:, lanes], NT)


def turn(own, pair, places):
    here = lambda rows: pl.BlockSpec((rows, WIDE), lambda j: (0, j))
    after = lambda rows: pl.BlockSpec((rows, WIDE), lambda j: (0, jnp.minimum(j + 1, CHIPS - 1)))
    after_map = pl.BlockSpec((8, WIDE), lambda j: (0, j + 1))
    return pl.pallas_call(
        turn_kernel,
        grid=(CHIPS,),
        out_shape=jax.ShapeDtypeStruct((CHIPS, ROWS, WIDE), F32),
        in_specs=[here(8), after_map, here(ROWS), after(ROWS), here(ROWS), after(ROWS)],
        out_specs=pl.BlockSpec((1, ROWS, WIDE), lambda j: (j, 0, 0)),
        scratch_shapes=[pltpu.VMEM((WIDE, 2 * WIDE), F32), pltpu.VMEM((8, 2 * WIDE), jnp.int32)],
        cost_estimate=pl.CostEstimate(flops=400_000_000, bytes_accessed=15_000_000, transcendentals=0),
        name="turn",
    )(places, places, own, own, pair, pair)


def child_kernel(
    order_ref, map_here, map_next, map_own, map_after, here_ref, next_ref, own_ref, after_ref,
    inverse_ref, moved_here, moved_next, panel_ref, lead_ref, turned_ref, self_ref, weights, window, places,
):
    step = pl.program_id(0)
    grid_rank = lax.axis_index("grid")
    count = len(TURNED)

    @pl.when(step == 0)
    def _():
        inverse = inverse_ref[...]
        mine = pl.ds(pl.multiple_of((grid_rank % 2) * ROWS, 64), ROWS)
        panel_ref[...] = exact(own_ref[mine, :], inverse, NT)
        wanted = grid_rank * ROWS + lax.broadcasted_iota(jnp.int32, (ROWS, WIDE), 0)
        picked = pick((wanted == map_own[:1, :]).astype(F32).astype(BF16), own_ref[...], NN)
        picked += pick((wanted == map_after[:1, :]).astype(F32).astype(BF16), after_ref[...], NN)
        weights[...] = exact(exact(picked, inverse, NT), inverse, NN)

    w = weights[...]
    window[:, :WIDE] = moved_here[0] - product(w, here_ref[...], NT)
    window[:, WIDE:] = moved_next[0] - product(w, next_ref[...], NT)
    places[:, :WIDE] = map_here[...]
    places[:, WIDE:] = map_next[...]
    first = order_ref[step] * WIDE

    def columns(low, wide):
        wanted = first + low + lax.broadcasted_iota(jnp.int32, (wide, wide + 256), 0)
        one_hot = (wanted == places[:1, low : low + wide + 256]).astype(F32).astype(BF16)
        high, rest = split(window[:, low : low + wide + 256])
        return dot(high, one_hot, NT) + dot(rest, one_hot, NT)

    result = jnp.concatenate([columns(0, 256), columns(256, 128)], axis=1)

    @pl.when(step == 0)
    def _():
        lead_ref[...] = result

    @pl.when((step > 0) & (step <= count))
    def _():
        turned_ref[0] = result

    @pl.when(step > count)
    def _():
        self_ref[0] = result


def child_schur(order, places, columns, inverse, moved):
    last = CHIPS - 1
    count = len(TURNED)
    total = 1 + count + len(SELF)

    def block(shape, index):
        return pl.BlockSpec(shape, index)

    here = lambda i, order: order[i]
    after = lambda i, order: jnp.minimum(order[i] + 1, last)
    own = lambda i, order: order[total]
    own_after = lambda i, order: jnp.minimum(order[total] + 1, last)
    spec = pltpu.PrefetchScalarGridSpec(
        num_scalar_prefetch=1,
        grid=(total,),
        in_specs=[
            block((8, WIDE), lambda i, order: (0, order[i])),
            block((8, WIDE), lambda i, order: (0, order[i] + 1)),
            block((8, WIDE), lambda i, order: (0, order[total])),
            block((8, WIDE), lambda i, order: (0, order[total] + 1)),
            block((WIDE, PMAX), lambda i, order: (here(i, order), 0)),
            block((WIDE, PMAX), lambda i, order: (after(i, order), 0)),
            block((WIDE, PMAX), lambda i, order: (own(i, order), 0)),
            block((WIDE, PMAX), lambda i, order: (own_after(i, order), 0)),
            block((PMAX, PMAX), lambda i, order: (0, 0)),
            block((1, ROWS, WIDE), lambda i, order: (here(i, order), 0, 0)),
            block((1, ROWS, WIDE), lambda i, order: (after(i, order), 0, 0)),
        ],
        out_specs=(
            block((ROWS, PMAX), lambda i, order: (0, 0)),
            block((ROWS, WIDE), lambda i, order: (0, 0)),
            block((1, ROWS, WIDE), lambda i, order: (jnp.clip(i - 1, 0, count - 1), 0, 0)),
            block((1, ROWS, WIDE), lambda i, order: (jnp.clip(i - 1 - count, 0, SIDE - 1), 0, 0)),
        ),
        scratch_shapes=[
            pltpu.VMEM((ROWS, PMAX), F32),
            pltpu.VMEM((ROWS, 2 * WIDE), F32),
            pltpu.VMEM((8, 2 * WIDE), jnp.int32),
        ],
    )
    return pl.pallas_call(
        child_kernel,
        grid_spec=spec,
        out_shape=(
            jax.ShapeDtypeStruct((ROWS, PMAX), F32),
            jax.ShapeDtypeStruct((ROWS, WIDE), F32),
            jax.ShapeDtypeStruct((count, ROWS, WIDE), F32),
            jax.ShapeDtypeStruct((SIDE, ROWS, WIDE), F32),
        ),
        cost_estimate=pl.CostEstimate(flops=400_000_000, bytes_accessed=20_000_000, transcendentals=0),
        name="child_schur",
    )(order, places, places, places, places, columns, columns, columns, columns, inverse, moved, moved)


def parent_kernel(
    order_ref, pivots_ref, weight_ref, own_ref, here_ref, inverse_ref, self_ref, sum_ref, mirror_ref, front_ref,
    panel_ref, schur_ref, weights,
):
    step = pl.program_id(0)
    grid_rank = lax.axis_index("grid")
    count = len(TURNED)

    @pl.when(step == 0)
    def _():
        inverse = inverse_ref[...]
        panel = exact(own_ref[...], inverse, NT)
        panel_ref[...] = panel
        weights[...] = exact(panel, inverse, NN)

    total = front_ref[...] - product(weights[...], here_ref[...], NT)
    pivots = pivots_ref[0]
    rows = grid_rank * ROWS + lax.broadcasted_iota(jnp.int32, (ROWS, WIDE), 0)
    columns = order_ref[step] * WIDE + lax.broadcasted_iota(jnp.int32, (ROWS, WIDE), 1)
    keep = (rows >= pivots) & (columns >= pivots)

    @pl.when(step < count)
    def _():
        schur_ref[...] = jnp.where(keep, total + sum_ref[0], 0.0)

    @pl.when((step >= count) & (step < 2 * count))
    def _():
        mirror = jnp.concatenate([mirror_ref[0, 0], mirror_ref[0, 1]], axis=1)
        schur_ref[...] = jnp.where(keep, total + mirror, 0.0)

    @pl.when(step >= 2 * count)
    def _():
        result = total
        for child in range(SIDE):
            result = result + weight_ref[child] * self_ref[child, 0]
        schur_ref[...] = jnp.where(keep, result, 0.0)


def parent_schur(order, pivots, weights, own, columns, inverse, selves, sums, mirror, front):
    smem = pl.BlockSpec(memory_space=pltpu.SMEM)
    count = len(TURNED)
    spec = pltpu.PrefetchScalarGridSpec(
        num_scalar_prefetch=1,
        grid=(CHIPS,),
        in_specs=[
            smem,
            smem,
            pl.BlockSpec((ROWS, PMAX), lambda i, order: (0, 0)),
            pl.BlockSpec((WIDE, PMAX), lambda i, order: (order[i], 0)),
            pl.BlockSpec((PMAX, PMAX), lambda i, order: (0, 0)),
            pl.BlockSpec((SIDE, 1, ROWS, WIDE), lambda i, order: (0, jnp.clip(i - 2 * count, 0, SIDE - 1), 0, 0)),
            pl.BlockSpec((1, ROWS, WIDE), lambda i, order: (jnp.clip(i, 0, count - 1), 0, 0)),
            pl.BlockSpec((1, 2, ROWS, ROWS), lambda i, order: (jnp.clip(i - count, 0, count - 1), 0, 0, 0)),
            pl.BlockSpec((ROWS, WIDE), lambda i, order: (0, order[i])),
        ],
        out_specs=(
            pl.BlockSpec((ROWS, PMAX), lambda i, order: (0, 0)),
            pl.BlockSpec((ROWS, WIDE), lambda i, order: (0, order[i])),
        ),
        scratch_shapes=[pltpu.VMEM((ROWS, PMAX), F32)],
    )
    return pl.pallas_call(
        parent_kernel,
        grid_spec=spec,
        out_shape=(jax.ShapeDtypeStruct((ROWS, PMAX), F32), jax.ShapeDtypeStruct((ROWS, ORDER), F32)),
        cost_estimate=pl.CostEstimate(flops=400_000_000, bytes_accessed=30_000_000, transcendentals=0),
        name="parent_schur",
    )(order, pivots, weights, own, columns, inverse, selves, sums, mirror, front)


def on_device(child_fronts, parent_fronts, child_maps, parent_of, child_pivots, parent_pivots):
    front_group = lax.axis_index("front")
    chip = lax.axis_index("grid") // 2
    front_rows = child_fronts[0]
    child_map = child_maps[front_group]
    pivots = child_pivots[front_group]
    upper_pivots = parent_pivots[front_group]
    weights = (parent_of == front_group).astype(F32)
    groups = (front_group - jnp.arange(SIDE, dtype=jnp.int32)) % SIDE
    lead_weights = (parent_of[groups] == front_group).astype(F32)
    turned_chips = [shifted(chip, offset) for offset in TURNED]
    mirror_chips = [shifted(chip, offset, -1) for offset in TURNED]
    self_chips = [shifted(chip, offset) for offset in SELF]
    child_order = jnp.stack([0 * chip] + turned_chips + self_chips + [chip]).astype(jnp.int32)
    parent_order = jnp.stack(turned_chips + mirror_chips + self_chips).astype(jnp.int32)

    pair = lax.ppermute(front_rows, "grid", [(g, g ^ 1) for g in range(2 * CHIPS)])
    position = jnp.arange(ORDER, dtype=jnp.int32)
    line = jnp.where(position >= pivots, child_map, -1)
    line = jnp.pad(line, (0, 2 * WIDE), constant_values=-1)
    places = jnp.broadcast_to(line[None], (8, line.shape[0]))
    turned = turn(front_rows, pair, places)
    same_core = [[2 * c + k for c in range(CHIPS)] for k in range(2)]
    moved = lax.all_to_all(turned, "grid", 0, 0, axis_index_groups=same_core)

    own = jnp.where(position[:PMAX] < pivots, front_rows[:, :PMAX], 0.0)
    columns = gather_rows(own, 0)
    inverse = inverse_factor(pivots[None], columns)
    panel_rows, lead, turned_part, self_part = child_schur(child_order, places, columns, inverse, moved)

    upper_own = lead_columns(upper_pivots[None], lead_weights, lead, parent_fronts[0])
    turned_all = lax.all_gather(turned_part, "front", axis=0)
    self_all = lax.all_gather(self_part, "front", axis=0)
    upper_columns = gather_rows(upper_own, 1)
    upper_inverse = inverse_factor(upper_pivots[None], upper_columns)
    sums, mirror = fold(weights, turned_all)
    landed = mirror_blocks(mirror)
    upper_panel, upper_schur = parent_schur(
        parent_order, upper_pivots[None], weights, upper_own, upper_columns, upper_inverse,
        self_all, sums, landed, parent_fronts[0],
    )
    return (panel_rows[None], upper_panel[None], upper_schur[None])


def solution(mesh):
    in_specs = (P("front", "grid", None), P("front", "grid", None), P(), P(), P(), P())
    out_specs = (P("front", "grid", None), P("front", "grid", None), P("front", "grid", None))
    return jax.shard_map(
        on_device, mesh=mesh, in_specs=in_specs, out_specs=out_specs, check_vma=False
    )
```

time: 436 us -> 349 us (0.80)
  waiting for transfers between devices: 244 us -> 6.84 us
  Pallas kernels: 127 us -> 307 us
  other arithmetic: 21.2 us -> 3.97 us
  blocking collectives: 13.8 us -> 0 us
    all_gather x3 -> x2, waiting for transfers between devices: 211 us -> 0.02 us  [the longest x1 0.02 us: on_device(): self_all = lax.all_gather(self_part, 'front', axis=0)]
    pallas_call x4 -> x9, Pallas kernels: 109 us -> 289 us  [the longest x2 124 us: gather_rows(): pl.pallas_call(gather_kernel, out_shape=jax.ShapeDtypeStruct((ORDER, PMAX...]
    all_to_all x1, waiting for transfers between devices: 24.4 us -> 0.01 us  [on_device(): moved = lax.all_to_all(turned, 'grid', 0, 0, axis_index_groups=same_core)]
    all_gather x1 -> x0, blocking collectives: 13.8 us -> none  [on_device(): leading = lax.all_gather(schur[0, :, :PMAX], 'front', axis=0)]
    select_n x1 -> x2, other arithmetic: 8.73 us -> 1.63 us  [the longest x1 1.62 us: on_device(): own = jnp.where(position[:PMAX] < pivots, front_rows[:, :PMAX], 0.0)]
    mul x2 -> x0, other arithmetic: 5.7 us -> none  [the longest x1 4.08 us: on_device(): upper_own = upper_own * upper_mask[None, :]]
  transfers between devices with their start and end apart: 5 -> 4, of which waited for: 5 -> 1; matrix products, arithmetic and copies ran while one was open for 4% -> 2% of each run, Pallas kernels for 18% -> 73%
where the time goes in v2:
time: 349 us; the launch traced here: 344 us
  Pallas kernels  307 us (88%)
  between operations  14.4 us (4%)
  starting transfers between devices  7.56 us (2%)
  waiting for transfers between devices  6.84 us (2%)
  local copies, waits for them, and re-layouts  4.58 us (1%)
  other arithmetic  3.97 us (1%)
    pallas_call x2, Pallas kernels, gather_rows(): pl.pallas_call(gather_kernel, out_shape=jax.ShapeDtypeStruct((ORDER, PMAX...  124 us
    pallas_call x2, Pallas kernels, inverse_factor(): pl.pallas_call(cholesky_kernel, grid=(1,), out_shape=jax.ShapeDtypeStruct...  59.6 us
    pallas_call x1, Pallas kernels, mirror_blocks(): pl.pallas_call(mirror_kernel, out_shape=jax.ShapeDtypeStruct((count, 2, R...  39.5 us
    pallas_call x1, Pallas kernels, lead_columns(): pl.pallas_call(lead_kernel, grid=(1,), out_shape=jax.ShapeDtypeStruct((RO...  22.8 us
    pallas_call x1, Pallas kernels, parent_schur(): pl.pallas_call(parent_kernel, grid_spec=spec, out_shape=(jax.ShapeDtypeSt...  19.5 us
    pallas_call x1, Pallas kernels, child_schur(): pl.pallas_call(child_kernel, grid_spec=spec, out_shape=(jax.ShapeDtypeStr...  17.7 us
    pallas_call x1, Pallas kernels, turn(): pl.pallas_call(turn_kernel, grid=(CHIPS,), out_shape=jax.ShapeDtypeStruct...  17.5 us
    all_to_all x1, starting transfers between devices, on_device(): moved = lax.all_to_all(turned, 'grid', 0, 0, axis_index_groups=same_core)  7.2 us
  transfers between devices with their start and end apart: 4, of which 1 were waited for; matrix products, arithmetic and copies ran while one was open for 2% of the time, Pallas kernels for 73%

profile of v2, /device:TPU:0, one launch (start us, length us, event | category | flops | bytes accessed | tf_op | source)
XLA Modules:
  0.0 344.3 jit_solution(6746171140494557342)
XLA Ops:
  7.2 0.0 copy-start
  7.2 0.1 collective-permute-start
  7.3 1.2 dynamic_slice.9.pivots_ref
  8.5 0.0 copy-done
  8.6 0.7 fusion
  9.2 6.3 %collective-permute-done.pair_here.pair_next = f32[192,6144]{1,0:T(8,128)} collective-permute-done((f32[192,6144]{1,0:T(8,128)}, f32[192,6144]{1,0:T(8,128)}, u32[]{:S(2)}, u32[]{:S(2)}) %collective-permute-start) | collective-permute-done | bytes 4718624 | tf_op jit(solution)/shard_map/ppermute | solution.py:560
  15.5 0.7 broadcast_in_dim.29.map_here.map_next.map_own.map_after
  16.2 17.5 %turn.1 = f32[16,192,384]{2,1,0:T(8,128)} custom-call(s32[8,6912]{1,0:T(8,128)} %broadcast_in_dim.29.map_here.map_next.map_own.map_after, s32[8,6912]{1,0:T(8,128)} %broadcast_in_dim.29.map_here.map_next.map_own.map_after, f32[192,6144]{1,0:T(8,128)} %bitcast.29, f32[192,6144]{1,0:T(8,128)} %bitcast.30, ...), custom_call_target="tpu_custom_call" | custom-call | flops 400000000 | bytes 15000000 | tf_op jit(solution)/shard_map/turn/pallas_call | solution.py:362
  33.7 7.2 %all-to-all-start = ((f32[16,192,384]{2,1,0:T(8,128)}), f32[16,192,384]{2,1,0:T(8,128)}, u32[]{:S(2)}, u32[]{:S(2)}) async-start(f32[16,192,384]{2,1,0:T(8,128)} %turn.1), calls=%async_computation | async-start | bytes 9437184 | tf_op jit(solution)/shard_map/all_to_all | solution.py:567
  40.9 0.0 all-gather.7.cloned.1.call-start
  41.1 0.7 stack.78.order_ref
  41.8 0.6 add_compare_fusion
  42.5 1.6 slice_select_fusion.own_ref
  44.1 93.7 %gather_rows.2.block_ref.here_ref.next_ref.own_ref.after_ref = f32[6144,256]{1,0:T(8,128)} custom-call(f32[192,256]{1,0:T(8,128)} %slice_select_fusion.own_ref), custom_call_target="tpu_custom_call" | custom-call | flops 400000000 | bytes 6300000 | tf_op jit(solution)/shard_map/gather_rows/pallas_call | solution.py:203
  137.8 29.8 %inverse_factor.2.inverse_ref = f32[256,256]{1,0:T(8,128)} custom-call(s32[1]{0:T(128)} %dynamic_slice.9.pivots_ref, f32[6144,256]{1,0:T(8,128)} %gather_rows.2.block_ref.here_ref.next_ref.own_ref.after_ref), custom_call_target="tpu_custom_call" | custom-call | flops 400000000 | bytes 524288 | tf_op jit(solution)/shard_map/inverse_factor/pallas_call | solution.py:105
  167.6 0.0 copy-start.2
  167.6 0.0 copy-start.1
  167.6 0.0 all-to-all-done.moved_here.moved_next
  167.6 17.7 %child_schur.1 = (f32[192,256]{1,0:T(8,128)}, f32[192,384]{1,0:T(8,128)}, f32[6,192,384]{2,1,0:T(8,128)}, f32[4,192,384]{2,1,0:T(8,128)}) custom-call(s32[12]{0:T(128)} %stack.78.order_ref, s32[8,6912]{1,0:T(8,128)} %broadcast_in_dim.29.map_here.map_next.map_own.map_after, s32[8,6912]{1,0:T(8,128)} %broadcast_in_dim.29.map_here.map_next.map_own.map_after, ...), custom_call_target="tpu_custom_call" | custom-call | flops 400000000 | bytes 20000000 | tf_op jit(solution)/shard_map/child_schur/pallas_call | solution.py:460
  185.3 0.0 all-gather.7.cloned.1.call-update
  185.3 0.2 all-gather.5.cloned.1.call-start
  185.6 0.5 all-gather.5.cloned.1.call-update
  186.2 0.0 copy-done.2
  186.2 0.6 dynamic_slice.11.pivots_ref
  186.9 0.0 copy-done.1
  186.9 0.6 gather_fusion
  187.5 0.6 stack.85.order_ref
  188.2 0.5 compare_convert_fusion.1.weight_ref
  188.7 0.5 compare_convert_fusion.weight_ref
  189.2 22.8 %lead_columns.1.own_ref = f32[192,256]{1,0:T(8,128)} custom-call(s32[1]{0:T(128)} %dynamic_slice.11.pivots_ref, f32[4]{0:T(128)} %compare_convert_fusion.weight_ref, f32[192,384]{1,0:T(8,128)} %get-tuple-element.12.lead_ref, f32[192,6144]{1,0:T(8,128)} %bitcast.32), custom_call_target="tpu_custom_call" | custom-call | flops 200000000 | bytes 1000000 | tf_op jit(solution)/shard_map/lead_columns/pallas_call | solution.py:238
  212.0 30.0 %gather_rows.3.block_ref.here_ref = f32[6144,256]{1,0:T(8,128)} custom-call(f32[192,256]{1,0:T(8,128)} %lead_columns.1.own_ref), custom_call_target="tpu_custom_call" | custom-call | flops 400000000 | bytes 6300000 | tf_op jit(solution)/shard_map/gather_rows/pallas_call | solution.py:203
  242.1 29.8 %inverse_factor.3.inverse_ref = f32[256,256]{1,0:T(8,128)} custom-call(s32[1]{0:T(128)} %dynamic_slice.11.pivots_ref, f32[6144,256]{1,0:T(8,128)} %gather_rows.3.block_ref.here_ref), custom_call_target="tpu_custom_call" | custom-call | flops 400000000 | bytes 524288 | tf_op jit(solution)/shard_map/inverse_factor/pallas_call | solution.py:105
  271.8 0.0 all-gather.7.cloned.1.call-done
  271.8 6.7 %fold.1 = (f32[6,192,384]{2,1,0:T(8,128)}, f32[6,2,192,192]{3,2,1,0:T(8,128)}) custom-call(f32[4]{0:T(128)} %compare_convert_fusion.1.weight_ref, f32[4,6,192,384]{3,2,1,0:T(8,128)} %bitcast.34), custom_call_target="tpu_custom_call" | custom-call | flops 100000000 | bytes 12000000 | tf_op jit(solution)/shard_map/fold/pallas_call | solution.py:271
  278.5 39.5 %mirror_blocks.1.mirror_ref = f32[6,2,192,192]{3,2,1,0:T(8,128)} custom-call(f32[6,2,192,192]{3,2,1,0:T(8,128)} %get-tuple-element.16.mirror_ref), custom_call_target="tpu_custom_call" | custom-call | flops 400000000 | bytes 5000000 | tf_op jit(solution)/shard_map/mirror_blocks/pallas_call | solution.py:328
  318.0 0.0 all-gather.5.cloned.1.call-done
  318.0 19.5 %parent_schur.1 = (f32[192,256]{1,0:T(8,128)}, f32[192,6144]{1,0:T(8,128)}) custom-call(s32[16]{0:T(128)} %stack.85.order_ref, s32[1]{0:T(128)} %dynamic_slice.11.pivots_ref, f32[4]{0:T(128)} %compare_convert_fusion.1.weight_ref, f32[192,256]{1,0:T(8,128)} %lead_columns.1.own_ref, f32[6144,256]{1,0:T(8,128)} %gather_rows.3.block_ref.here_ref, ...), custom_call_target="tpu_custom_call" | custom-call | flops 400000000 | bytes 30000000 | tf_op jit(solution)/shard_map/parent_schur/pallas_call | solution.py:535
  (4 shorter events, 0.0 us)
Async XLA Ops:
  7.2 1.4 copy-start
  7.2 8.3 %collective-permute-start = (f32[192,6144]{1,0:T(8,128)}, f32[192,6144]{1,0:T(8,128)}, u32[]{:S(2)}, u32[]{:S(2)}) collective-permute-start(f32[192,6144]{1,0:T(8,128)} %bitcast.28), channel_id=1, source_target_pairs={{0,1},{1,0},{2,3},{3,2},{4,5},{5,4},{6,7},{7,6},{8,9},{9,8},{10,11... | collective-permute-start | bytes 14155784 | tf_op jit(solution)/shard_map/ppermute | solution.py:560
  33.7 133.9 %all-to-all-start = ((f32[16,192,384]{2,1,0:T(8,128)}), f32[16,192,384]{2,1,0:T(8,128)}, u32[]{:S(2)}, u32[]{:S(2)}) async-start(f32[16,192,384]{2,1,0:T(8,128)} %turn.1), calls=%async_computation | async-start | bytes 9437184 | tf_op jit(solution)/shard_map/all_to_all | solution.py:567
  40.9 230.9 %all-gather.7.cloned.1.call-start = ((), (), s32[]{:S(2)}) async-start(), calls=%async_computation.2 | async-start | bytes 8847360 | tf_op jit(solution)/shard_map/all_gather | solution.py:575
  167.6 18.6 %copy-start.2 = (s32[4]{0:T(128)S(1)}, s32[4]{0:T(128)}, u32[]{:S(2)}) copy-start(s32[4]{0:T(128)} %param.11) | copy-start | bytes 52
  167.6 19.3 %copy-start.1 = (s32[4]{0:T(128)S(1)}, s32[4]{0:T(128)}, u32[]{:S(2)}) copy-start(s32[4]{0:T(128)} %param.9) | copy-start | bytes 52
  185.3 132.6 %all-gather.5.cloned.1.call-start = ((), (), s32[]{:S(2)}) async-start(), calls=%async_computation.1 | async-start | bytes 5898240 | tf_op jit(solution)/shard_map/all_gather | solution.py:576
Sparse Core Ops, SparseCore 0:
  185.5 77.3 all-gather.6
  264.5 50.7 all-gather.4

commit v3 on v2

--- a/solution.py
+++ b/solution.py
@@ -14,6 +14,7 @@
 WIDE = 384
 ORDER = 6144
 BASE = 32
+GROUP = 8
 LEAD = 256
 MESH = pl.DeviceIdType.MESH
 SELF = ((0, 0), (0, 2), (2, 0), (2, 2))
@@ -87,10 +88,19 @@
         last = first + BASE
         diagonal = work[first:last, first:last]
         both = jnp.concatenate([diagonal, eye, jnp.zeros((BASE, 128 - 2 * BASE), F32)], axis=1)
-        for k in range(BASE - 1):
-            column = jnp.where(small_rows > k, both[:, k : k + 1], 0.0)
-            row = both[k : k + 1, :]
-            both = both - column * (row / row[:, k : k + 1])
+        for group in range(0, BASE, GROUP):
+            columns_of = [jnp.broadcast_to(both[:, group + i : group + i + 1], (BASE, 128)) for i in range(GROUP)]
+            rows_of = [both[group + i : group + i + 1, :] for i in range(GROUP)]
+            for i in range(GROUP):
+                k = group + i
+                below = jnp.where(small_rows > k, columns_of[i], 0.0)
+                inverse_pivot = 1.0 / columns_of[i][k : k + 1, :]
+                scaled = rows_of[i] * inverse_pivot
+                for j in range(i + 1, GROUP):
+                    entry = columns_of[i][group + j : group + j + 1, :]
+                    columns_of[j] = columns_of[j] - below * (entry * inverse_pivot)
+                    rows_of[j] = rows_of[j] - entry * scaled
+                both = both - below * scaled
         pivot_values = jnp.sum(both[:, :BASE] * eye, axis=1, keepdims=True)
         inverse = both[:, BASE : 2 * BASE] / jnp.sqrt(pivot_values)
         strip = exact(inverse, work[first:last, :], NN)
@@ -98,7 +108,7 @@
         if last < PMAX:
             update = exact(strip[:, :PMAX], strip, TN)
             work[last:, :] = work[last:, :] - update[last:, :]
-    inverse_ref[...] = work[:, PMAX:]
+    inverse_ref[...] = jnp.where(rows < pivots, work[:, PMAX:], 0.0)
 
 
 def inverse_factor(pivots, columns):
@@ -114,7 +124,7 @@
     )(pivots, columns)
 
 
-def gather_kernel(own_ref, all_ref, local_sem, send_sems, recv_sems):
+def gather_stages(own_ref, all_ref, local_sem, send_sems, recv_sems):
     rank = lax.axis_index("grid")
     core = rank % 2
     chip = rank // 2
@@ -156,19 +166,24 @@
         send(4 + dp, rows(dp, 0), s_up)
         send(8 + dp, rows(dp, 0), s_down)
 
-    send(0, rows(0, 0), p_up, own_ref)
-    send(1, rows(0, 0), p_down, own_ref)
-    send(4, rows(0, 0), s_up, own_ref)
-    send(8, rows(0, 0), s_down, own_ref)
-    across(0, 0, own_ref)
-    arrived(0, rows(3, 0))
-    send(2, rows(3, 0, 0), p_up)
-    sideways(3)
-    across(3, 0)
-    arrived(1, rows(1, 0))
-    send(3, rows(1, 0, 1), p_down)
-    sideways(1)
-    across(1, 0)
+    def begin():
+        send(0, rows(0, 0), p_up, own_ref)
+        send(1, rows(0, 0), p_down, own_ref)
+        send(4, rows(0, 0), s_up, own_ref)
+        send(8, rows(0, 0), s_down, own_ref)
+        across(0, 0, own_ref)
+
+    def from_below():
+        arrived(0, rows(3, 0))
+        send(2, rows(3, 0, 0), p_up)
+        sideways(3)
+        across(3, 0)
+
+    def from_above():
+        arrived(1, rows(1, 0))
+        send(3, rows(1, 0, 1), p_down)
+        sideways(1)
+        across(1, 0)
 
     def pass_on(dp):
         arrived(4 + dp, rows(dp, 3))
@@ -178,25 +193,36 @@
         send(16 + dp, rows(dp, 1, 1), s_down)
         across(dp, 1)
 
-    pass_on(0)
-    arrived(2, rows(2, 0, 0))
-    arrived(3, rows(2, 0, 1))
-    sideways(2)
-    across(2, 0)
-    for dp in (3, 1, 2):
-        pass_on(dp)
-    for dp in (0, 3, 1, 2):
+    def opposite():
+        arrived(2, rows(2, 0, 0))
+        arrived(3, rows(2, 0, 1))
+        sideways(2)
+        across(2, 0)
+
+    def complete(dp):
         arrived(12 + dp, rows(dp, 2, 0))
         arrived(16 + dp, rows(dp, 2, 1))
         across(dp, 2)
-    for copy in copies:
-        copy.wait_send()
-    for dp in range(SIDE):
-        for ds in range(SIDE):
-            chip_there = ((s + dp) % SIDE) * (4 - 3 * core) + ((p + ds) % SIDE) * (1 + 3 * core)
-            first = (2 * chip_there + 1 - core) * ROWS
-            arrived(20 + 4 * dp + ds, pl.ds(pl.multiple_of(first, 64), ROWS))
-    here.wait()
+
+    def finish():
+        for copy in copies:
+            copy.wait_send()
+        for dp in range(SIDE):
+            for ds in range(SIDE):
+                chip_there = ((s + dp) % SIDE) * (4 - 3 * core) + ((p + ds) % SIDE) * (1 + 3 * core)
+                first = (2 * chip_there + 1 - core) * ROWS
+                arrived(20 + 4 * dp + ds, pl.ds(pl.multiple_of(first, 64), ROWS))
+        here.wait()
+
+    steps = [begin, from_below, from_above, functools.partial(pass_on, 0), opposite]
+    steps += [functools.partial(pass_on, dp) for dp in (3, 1, 2)]
+    steps += [functools.partial(complete, dp) for dp in (0, 3, 1, 2)]
+    return steps + [finish]
+
+
+def gather_kernel(own_ref, all_ref, local_sem, send_sems, recv_sems):
+    for step in gather_stages(own_ref, all_ref, local_sem, send_sems, recv_sems):
+        step()
 
 
 def gather_rows(own, collective_id):
@@ -216,7 +242,7 @@
     )(own)
 
 
-def lead_kernel(pivots_ref, weight_ref, lead_ref, front_ref, out_ref, landing, send_sems, recv_sems):
+def lead_kernel(weight_ref, lead_ref, front_ref, out_ref, landing, send_sems, recv_sems):
     group = lax.axis_index("front")
     others = [{"front": (group + d) % SIDE} for d in range(1, SIDE)]
     greet(others)
@@ -224,23 +250,21 @@
     copies = [remote(lead_ref.at[:, pl.ds(0, LEAD)], landing.at[d], sems, d, others[d]) for d in range(SIDE - 1)]
     for copy in copies:
         copy.start()
-    pivots = pivots_ref[0]
     total = front_ref[...] + weight_ref[0] * lead_ref[:, :LEAD]
     for d in range(SIDE - 1):
         copies[d].wait()
         total = total + weight_ref[d + 1] * landing[d]
-    columns = lax.broadcasted_iota(jnp.int32, (ROWS, LEAD), 1)
-    out_ref[...] = jnp.where(columns < pivots, total, 0.0)
-
-
-def lead_columns(pivots, weights, lead, front):
+    out_ref[...] = total
+
+
+def lead_columns(weights, lead, front):
     smem = pl.BlockSpec(memory_space=pltpu.SMEM)
     return pl.pallas_call(
         lead_kernel,
         grid=(1,),
         out_shape=jax.ShapeDtypeStruct((ROWS, LEAD), F32),
         in_specs=[
-            smem, smem,
+            smem,
             pl.BlockSpec((ROWS, WIDE), lambda j: (0, 0)),
             pl.BlockSpec((ROWS, LEAD), lambda j: (0, 0)),
         ],
@@ -253,7 +277,7 @@
         compiler_params=pltpu.CompilerParams(collective_id=2, has_side_effects=True),
         cost_estimate=pl.CostEstimate(flops=200_000_000, bytes_accessed=1_000_000, transcendentals=0),
         name="lead_columns",
-    )(pivots, weights, lead, front)
+    )(weights, lead, front)
 
 
 def fold_kernel(weight_ref, children_ref, sum_ref, mirror_ref):
@@ -337,38 +361,89 @@
     )(mirror)
 
 
-def turn_kernel(map_here, map_next, own_here, own_next, pair_here, pair_next, out_ref, window, places):
-    core = lax.axis_index("grid") % 2
-    block = pl.program_id(0)
-    own = pl.ds(pl.multiple_of(core * ROWS, 64), ROWS)
-    pair = pl.ds(pl.multiple_of((1 - core) * ROWS, 64), ROWS)
-    window[own, :WIDE] = own_here[...]
-    window[own, WIDE:] = own_next[...]
-    window[pair, :WIDE] = pair_here[...]
-    window[pair, WIDE:] = pair_next[...]
-    places[:, :WIDE] = map_here[...]
-    places[:, WIDE:] = map_next[...]
-    lanes = pl.ds(pl.multiple_of(core * 128, 128), 512)
-    first = block * WIDE + core * ROWS
-    wanted = first + lax.broadcasted_iota(jnp.int32, (ROWS, 512), 0)
-    one_hot = (wanted == places[:1, lanes]).astype(F32).astype(BF16)
-    out_ref[0] = pick(one_hot, window[:, lanes], NT)
-
-
-def turn(own, pair, places):
-    here = lambda rows: pl.BlockSpec((rows, WIDE), lambda j: (0, j))
-    after = lambda rows: pl.BlockSpec((rows, WIDE), lambda j: (0, jnp.minimum(j + 1, CHIPS - 1)))
-    after_map = pl.BlockSpec((8, WIDE), lambda j: (0, j + 1))
-    return pl.pallas_call(
-        turn_kernel,
-        grid=(CHIPS,),
-        out_shape=jax.ShapeDtypeStruct((CHIPS, ROWS, WIDE), F32),
-        in_specs=[here(8), after_map, here(ROWS), after(ROWS), here(ROWS), after(ROWS)],
-        out_specs=pl.BlockSpec((1, ROWS, WIDE), lambda j: (j, 0, 0)),
-        scratch_shapes=[pltpu.VMEM((WIDE, 2 * WIDE), F32), pltpu.VMEM((8, 2 * WIDE), jnp.int32)],
-        cost_estimate=pl.CostEstimate(flops=400_000_000, bytes_accessed=15_000_000, transcendentals=0),
-        name="turn",
-    )(places, places, own, own, pair, pair)
+def front_kernel(
+    places_ref, rows_ref, own_ref, all_ref, turned_ref, both, local_sem, send_sems, recv_sems, own_sems, out_sems, in_sems
+):
+    rank = lax.axis_index("grid")
+    core = rank % 2
+    steps = gather_stages(own_ref, all_ref, local_sem, send_sems, recv_sems)
+    sibling = {"grid": rank + 1 - 2 * core}
+    mine = pl.ds(pl.multiple_of(core * ROWS, 64), ROWS)
+
+    def local(j):
+        lanes = pl.ds(pl.multiple_of(j * WIDE, 128), WIDE)
+        return pltpu.make_async_copy(rows_ref.at[:, lanes], both.at[mine, lanes], own_sems.at[j])
+
+    def pair(j):
+        lanes = pl.ds(pl.multiple_of(j * WIDE, 128), WIDE)
+        return pltpu.make_async_remote_copy(
+            src_ref=rows_ref.at[:, lanes], dst_ref=both.at[mine, lanes],
+            send_sem=out_sems.at[j], recv_sem=in_sems.at[j], device_id=sibling, device_id_type=MESH,
+        )
+
+    steps[0]()
+    for j in range(CHIPS):
+        pair(j).start()
+        local(j).start()
+
+    def here(j):
+        local(j).wait()
+        pair(j).wait()
+
+    def work(j, carry):
+        @pl.when(j < CHIPS - 1)
+        def _():
+            here(j + 1)
+
+        first = j * WIDE + core * ROWS
+        start = jnp.minimum(j * WIDE + core * 128, ORDER - 512)
+        lanes = pl.ds(pl.multiple_of(start, 128), 512)
+        wanted = first + lax.broadcasted_iota(jnp.int32, (ROWS, 512), 0)
+        one_hot = (wanted == places_ref[:1, lanes]).astype(F32).astype(BF16)
+        turned_ref[j] = pick(one_hot, both[:, lanes], NT)
+        return carry
+
+    here(0)
+    done = 0
+    rest = steps[1:-1]
+    for index, step in enumerate(rest):
+        until = (CHIPS * (index + 1)) // len(rest)
+        lax.fori_loop(done, until, work, 0)
+        done = until
+        step()
+    steps[-1]()
+
+
+def front(rows, places):
+    return pl.pallas_call(
+        front_kernel,
+        grid=(1,),
+        out_shape=(
+            jax.ShapeDtypeStruct((ORDER, PMAX), F32),
+            jax.ShapeDtypeStruct((CHIPS, ROWS, WIDE), F32),
+        ),
+        in_specs=[
+            pl.BlockSpec(places.shape, lambda i: (0, 0)),
+            pl.BlockSpec(memory_space=pl.ANY),
+            pl.BlockSpec((ROWS, PMAX), lambda i: (0, 0)),
+        ],
+        out_specs=(
+            pl.BlockSpec((ORDER, PMAX), lambda i: (0, 0)),
+            pl.BlockSpec((CHIPS, ROWS, WIDE), lambda i: (0, 0, 0)),
+        ),
+        scratch_shapes=[
+            pltpu.VMEM((WIDE, ORDER), F32),
+            pltpu.SemaphoreType.DMA,
+            pltpu.SemaphoreType.DMA((36,)),
+            pltpu.SemaphoreType.DMA((36,)),
+            pltpu.SemaphoreType.DMA((CHIPS,)),
+            pltpu.SemaphoreType.DMA((CHIPS,)),
+            pltpu.SemaphoreType.DMA((CHIPS,)),
+        ],
+        compiler_params=pltpu.CompilerParams(collective_id=0, has_side_effects=True),
+        cost_estimate=pl.CostEstimate(flops=400_000_000, bytes_accessed=25_000_000, transcendentals=0),
+        name="front",
+    )(places, rows, rows)
 
 
 def child_kernel(
@@ -557,21 +632,18 @@
     child_order = jnp.stack([0 * chip] + turned_chips + self_chips + [chip]).astype(jnp.int32)
     parent_order = jnp.stack(turned_chips + mirror_chips + self_chips).astype(jnp.int32)
 
-    pair = lax.ppermute(front_rows, "grid", [(g, g ^ 1) for g in range(2 * CHIPS)])
     position = jnp.arange(ORDER, dtype=jnp.int32)
     line = jnp.where(position >= pivots, child_map, -1)
     line = jnp.pad(line, (0, 2 * WIDE), constant_values=-1)
     places = jnp.broadcast_to(line[None], (8, line.shape[0]))
-    turned = turn(front_rows, pair, places)
+    columns, turned = front(front_rows, places)
     same_core = [[2 * c + k for c in range(CHIPS)] for k in range(2)]
     moved = lax.all_to_all(turned, "grid", 0, 0, axis_index_groups=same_core)
 
-    own = jnp.where(position[:PMAX] < pivots, front_rows[:, :PMAX], 0.0)
-    columns = gather_rows(own, 0)
     inverse = inverse_factor(pivots[None], columns)
     panel_rows, lead, turned_part, self_part = child_schur(child_order, places, columns, inverse, moved)
 
-    upper_own = lead_columns(upper_pivots[None], lead_weights, lead, parent_fronts[0])
+    upper_own = lead_columns(lead_weights, lead, parent_fronts[0])
     turned_all = lax.all_gather(turned_part, "front", axis=0)
     self_all = lax.all_gather(self_part, "front", axis=0)
     upper_columns = gather_rows(upper_own, 1)

time: 349 us -> 295 us (0.85)
  Pallas kernels: 307 us -> 203 us
  waiting for transfers between devices: 6.84 us -> 63.4 us
    pallas_call x2 -> x1, Pallas kernels: 124 us -> 39.1 us  [gather_rows(): pl.pallas_call(gather_kernel, out_shape=jax.ShapeDtypeStruct((ORDER, PMAX...]
    all_to_all x1, waiting for transfers between devices: 0.01 us -> 48.4 us  [on_device(): moved = lax.all_to_all(turned, 'grid', 0, 0, axis_index_groups=same_core)]
    pallas_call x2, Pallas kernels: 59.6 us -> 30.3 us  [inverse_factor(): pl.pallas_call(cholesky_kernel, grid=(1,), out_shape=jax.ShapeDtypeStruct...]
    pallas_call x1, Pallas kernels: 17.5 us -> 31.6 us  [front(): pl.pallas_call(front_kernel, grid=(1,), out_shape=(jax.ShapeDtypeStruct((...]
    all_gather x1, waiting for transfers between devices: 0.01 us -> 7.71 us  [on_device(): turned_all = lax.all_gather(turned_part, 'front', axis=0)]
    pallas_call x1, Pallas kernels: 22.8 us -> 15.8 us  [lead_columns(): pl.pallas_call(lead_kernel, grid=(1,), out_shape=jax.ShapeDtypeStruct((RO...]
    all_gather x1, waiting for transfers between devices: 0.02 us -> 6.73 us  [on_device(): self_all = lax.all_gather(self_part, 'front', axis=0)]
    ppermute x1 -> x0, waiting for transfers between devices: 6.28 us -> none  [on_device(): lax.ppermute(front_rows, 'grid', [(g, g ^ 1) for g in range(2 * CHIPS)])]
  transfers between devices with their start and end apart: 4 -> 3, of which waited for: 1 -> 3; matrix products, arithmetic and copies ran while one was open for 2% -> 1% of each run, Pallas kernels for 73% -> 46%
where the time goes in v3:
time: 295 us; the launch traced here: 293 us
  Pallas kernels  203 us (69%)
  waiting for transfers between devices  63.4 us (21%)
  between operations  14.4 us (5%)
  starting transfers between devices  6.11 us (2%)
  local copies, waits for them, and re-layouts  4.62 us (2%)
    all_to_all x1, waiting for transfers between devices, on_device(): moved = lax.all_to_all(turned, 'grid', 0, 0, axis_index_groups=same_core)  48.4 us
    pallas_call x1, Pallas kernels, mirror_blocks(): pl.pallas_call(mirror_kernel, out_shape=jax.ShapeDtypeStruct((count, 2, R...  42.4 us
    pallas_call x1, Pallas kernels, gather_rows(): pl.pallas_call(gather_kernel, out_shape=jax.ShapeDtypeStruct((ORDER, PMAX...  39.1 us
    pallas_call x1, Pallas kernels, front(): pl.pallas_call(front_kernel, grid=(1,), out_shape=(jax.ShapeDtypeStruct((...  31.6 us
    pallas_call x2, Pallas kernels, inverse_factor(): pl.pallas_call(cholesky_kernel, grid=(1,), out_shape=jax.ShapeDtypeStruct...  30.3 us
    pallas_call x1, Pallas kernels, parent_schur(): pl.pallas_call(parent_kernel, grid_spec=spec, out_shape=(jax.ShapeDtypeSt...  19.5 us
    pallas_call x1, Pallas kernels, child_schur(): pl.pallas_call(child_kernel, grid_spec=spec, out_shape=(jax.ShapeDtypeStr...  17.6 us
    pallas_call x1, Pallas kernels, lead_columns(): pl.pallas_call(lead_kernel, grid=(1,), out_shape=jax.ShapeDtypeStruct((RO...  15.8 us
  transfers between devices with their start and end apart: 3, of which 3 were waited for; matrix products, arithmetic and copies ran while one was open for 1% of the time, Pallas kernels for 46%

profile of v3, /device:TPU:0, one launch (start us, length us, event | category | flops | bytes accessed | tf_op | source)
XLA Modules:
  0.0 292.9 jit_solution(15136382721679622546)
XLA Ops:
  7.2 0.0 copy-start
  7.2 1.3 dynamic_slice.9.pivots_ref
  8.5 0.0 copy-done
  8.5 0.7 fusion
  9.2 0.7 broadcast_in_dim.21.places_ref.map_here.map_next.map_own.map_after
  9.9 31.6 %front.1 = (f32[6144,256]{1,0:T(8,128)}, f32[16,192,384]{2,1,0:T(8,128)}) custom-call(s32[8,6912]{1,0:T(8,128)} %broadcast_in_dim.21.places_ref.map_here.map_next.map_own.map_after, f32[192,6144]{1,0:T(8,128)} %bitcast.28, f32[192,6144]{1,0:T(8,128)} %bitcast.29), custom_call_target="tpu_custom_call" | custom-call | flops 400000000 | bytes 25000000 | tf_op jit(solution)/shard_map/front/pallas_call | solution.py:418
  41.4 5.6 %all-to-all-start = ((f32[16,192,384]{2,1,0:T(8,128)}), f32[16,192,384]{2,1,0:T(8,128)}, u32[]{:S(2)}, u32[]{:S(2)}) async-start(f32[16,192,384]{2,1,0:T(8,128)} %get-tuple-element.14), calls=%async_computation | async-start | bytes 9437184 | tf_op jit(solution)/shard_map/all_to_all | solution.py:641
  47.1 0.2 all-gather.7.cloned.1.call-start
  47.5 0.7 stack.78.order_ref
  48.1 15.1 %inverse_factor.2.inverse_ref = f32[256,256]{1,0:T(8,128)} custom-call(s32[1]{0:T(128)} %dynamic_slice.9.pivots_ref, f32[6144,256]{1,0:T(8,128)} %get-tuple-element.13.block_ref.here_ref.next_ref.own_ref.after_ref), custom_call_target="tpu_custom_call" | custom-call | flops 400000000 | bytes 524288 | tf_op jit(solution)/shard_map/inverse_factor/pallas_call | solution.py:115
  63.3 0.0 copy-start.2
  63.3 0.0 copy-start.1
  63.3 48.4 %all-to-all-done.moved_here.moved_next = f32[16,192,384]{2,1,0:T(8,128)} async-done(((f32[16,192,384]{2,1,0:T(8,128)}), f32[16,192,384]{2,1,0:T(8,128)}, u32[]{:S(2)}, u32[]{:S(2)}) %all-to-all-start) | async-done | bytes 4718624 | tf_op jit(solution)/shard_map/all_to_all | solution.py:641
  111.7 17.6 %child_schur.1 = (f32[192,256]{1,0:T(8,128)}, f32[192,384]{1,0:T(8,128)}, f32[6,192,384]{2,1,0:T(8,128)}, f32[4,192,384]{2,1,0:T(8,128)}) custom-call(s32[12]{0:T(128)} %stack.78.order_ref, s32[8,6912]{1,0:T(8,128)} %broadcast_in_dim.21.places_ref.map_here.map_next.map_own.map_after, ...), custom_call_target="tpu_custom_call" | custom-call | flops 400000000 | bytes 20000000 | tf_op jit(solution)/shard_map/child_schur/pallas_call | solution.py:535
  129.3 0.0 all-gather.7.cloned.1.call-update
  129.3 0.3 all-gather.5.cloned.1.call-start
  129.6 0.5 all-gather.5.cloned.1.call-update
  130.2 0.0 copy-done.2
  130.2 0.6 dynamic_slice.11.pivots_ref
  130.9 0.0 copy-done.1
  130.9 0.6 gather_fusion
  131.5 0.6 stack.85.order_ref
  132.2 0.5 compare_convert_fusion.1.weight_ref
  132.7 0.5 compare_convert_fusion.weight_ref
  133.2 15.8 %lead_columns.1.own_ref = f32[192,256]{1,0:T(8,128)} custom-call(f32[4]{0:T(128)} %compare_convert_fusion.weight_ref, f32[192,384]{1,0:T(8,128)} %get-tuple-element.16.lead_ref, f32[192,6144]{1,0:T(8,128)} %bitcast.30), custom_call_target="tpu_custom_call" | custom-call | flops 200000000 | bytes 1000000 | tf_op jit(solution)/shard_map/lead_columns/pallas_call | solution.py:262
  149.0 39.1 %gather_rows.1.block_ref.here_ref = f32[6144,256]{1,0:T(8,128)} custom-call(f32[192,256]{1,0:T(8,128)} %lead_columns.1.own_ref), custom_call_target="tpu_custom_call" | custom-call | flops 400000000 | bytes 6300000 | tf_op jit(solution)/shard_map/gather_rows/pallas_call | solution.py:229
  188.1 15.1 %inverse_factor.3.inverse_ref = f32[256,256]{1,0:T(8,128)} custom-call(s32[1]{0:T(128)} %dynamic_slice.11.pivots_ref, f32[6144,256]{1,0:T(8,128)} %gather_rows.1.block_ref.here_ref), custom_call_target="tpu_custom_call" | custom-call | flops 400000000 | bytes 524288 | tf_op jit(solution)/shard_map/inverse_factor/pallas_call | solution.py:115
  203.3 7.7 %all-gather.7.cloned.1.call-done = f32[24,192,384]{2,1,0:T(8,128)} async-done(((f32[6,192,384]{2,1,0:T(8,128)}), f32[24,192,384]{2,1,0:T(8,128)}) %all-gather.7.cloned.1.call-update) | async-done | bytes 7077904 | tf_op jit(solution)/shard_map/all_gather | solution.py:647
  211.0 6.4 %fold.1 = (f32[6,192,384]{2,1,0:T(8,128)}, f32[6,2,192,192]{3,2,1,0:T(8,128)}) custom-call(f32[4]{0:T(128)} %compare_convert_fusion.1.weight_ref, f32[4,6,192,384]{3,2,1,0:T(8,128)} %bitcast.32), custom_call_target="tpu_custom_call" | custom-call | flops 100000000 | bytes 12000000 | tf_op jit(solution)/shard_map/fold/pallas_call | solution.py:295
  217.4 42.4 %mirror_blocks.1.mirror_ref = f32[6,2,192,192]{3,2,1,0:T(8,128)} custom-call(f32[6,2,192,192]{3,2,1,0:T(8,128)} %get-tuple-element.20.mirror_ref), custom_call_target="tpu_custom_call" | custom-call | flops 400000000 | bytes 5000000 | tf_op jit(solution)/shard_map/mirror_blocks/pallas_call | solution.py:352
  259.8 6.7 %all-gather.5.cloned.1.call-done = f32[16,192,384]{2,1,0:T(8,128)} async-done(((f32[4,192,384]{2,1,0:T(8,128)}), f32[16,192,384]{2,1,0:T(8,128)}) %all-gather.5.cloned.1.call-update) | async-done | bytes 4718608 | tf_op jit(solution)/shard_map/all_gather | solution.py:648
  266.6 19.5 %parent_schur.1 = (f32[192,256]{1,0:T(8,128)}, f32[192,6144]{1,0:T(8,128)}) custom-call(s32[16]{0:T(128)} %stack.85.order_ref, s32[1]{0:T(128)} %dynamic_slice.11.pivots_ref, f32[4]{0:T(128)} %compare_convert_fusion.1.weight_ref, f32[192,256]{1,0:T(8,128)} %lead_columns.1.own_ref, f32[6144,256]{1,0:T(8,128)} %gather_rows.1.block_ref.here_ref, ...), custom_call_target="tpu_custom_call" | custom-call | flops 400000000 | bytes 30000000 | tf_op jit(solution)/shard_map/parent_schur/pallas_call | solution.py:610
  (4 shorter events, 0.0 us)
Async XLA Ops:
  7.2 1.3 copy-start
  41.4 70.3 %all-to-all-start = ((f32[16,192,384]{2,1,0:T(8,128)}), f32[16,192,384]{2,1,0:T(8,128)}, u32[]{:S(2)}, u32[]{:S(2)}) async-start(f32[16,192,384]{2,1,0:T(8,128)} %get-tuple-element.14), calls=%async_computation | async-start | bytes 9437184 | tf_op jit(solution)/shard_map/all_to_all | solution.py:641
  47.1 163.9 %all-gather.7.cloned.1.call-start = ((), (), s32[]{:S(2)}) async-start(), calls=%async_computation.2 | async-start | bytes 8847360 | tf_op jit(solution)/shard_map/all_gather | solution.py:647
  63.3 66.9 %copy-start.2 = (s32[4]{0:T(128)S(1)}, s32[4]{0:T(128)}, u32[]{:S(2)}) copy-start(s32[4]{0:T(128)} %param.11) | copy-start | bytes 52
  63.3 67.6 %copy-start.1 = (s32[4]{0:T(128)S(1)}, s32[4]{0:T(128)}, u32[]{:S(2)}) copy-start(s32[4]{0:T(128)} %param.9) | copy-start | bytes 52
  129.3 137.2 %all-gather.5.cloned.1.call-start = ((), (), s32[]{:S(2)}) async-start(), calls=%async_computation.1 | async-start | bytes 5898240 | tf_op jit(solution)/shard_map/all_gather | solution.py:648
Sparse Core Ops, SparseCore 0:
  129.5 81.4 all-gather.6
  212.6 53.8 all-gather.4

commit v4 on v3

v4 whole, which is shorter than its diff:
```python
import functools

import jax
import jax.numpy as jnp
from jax import lax
from jax.experimental import pallas as pl
from jax.experimental.pallas import tpu as pltpu
from jax.sharding import PartitionSpec as P

PMAX = 256
CHIPS = 16
SIDE = 4
ROWS = 192
WIDE = 384
ORDER = 6144
BASE = 32
GROUP = 8
LEAD = 256
MESH = pl.DeviceIdType.MESH
SELF = ((0, 0), (0, 2), (2, 0), (2, 2))
TURNED = ((0, 1), (1, 0), (3, 3), (3, 1), (1, 2), (2, 3))
F32 = jnp.float32
BF16 = jnp.bfloat16
VMEM = pltpu.VMEM
NT = (((1,), (1,)), ((), ()))
NN = (((1,), (0,)), ((), ()))
TN = (((0,), (0,)), ((), ()))


def dot(a, b, dims):
    return lax.dot_general(a, b, dims, preferred_element_type=F32)


def split(a):
    high = a.astype(BF16)
    low = (a - high.astype(F32)).astype(BF16)
    return high, low


def product(a, b, dims):
    a_high, a_low = split(a)
    b_high, b_low = split(b)
    return dot(a_high, b_high, dims) + (dot(a_high, b_low, dims) + dot(a_low, b_high, dims))


def pick(one_hot, a, dims):
    a_high, a_low = split(a)
    return dot(one_hot, a_high, dims) + dot(one_hot, a_low, dims)


def exact(a, b, dims):
    return lax.dot_general(a, b, dims, precision=lax.Precision.HIGHEST, preferred_element_type=F32)


def shifted(chip, offset, sign=1):
    x = (chip // SIDE + sign * offset[0] + SIDE) % SIDE
    y = (chip % SIDE + sign * offset[1] + SIDE) % SIDE
    return x * SIDE + y


def remote(src, dst, sems, index, device):
    return pltpu.make_async_remote_copy(
        src_ref=src, dst_ref=dst, send_sem=sems[0].at[index], recv_sem=sems[1].at[index],
        device_id=device, device_id_type=MESH,
    )


def greet(devices, more=0):
    barrier = pltpu.get_barrier_semaphore()
    for device in devices:
        pl.semaphore_signal(barrier, inc=1, device_id=device, device_id_type=MESH)
    pl.semaphore_wait(barrier, len(devices) + more)


def cholesky_kernel(pivots_ref, block_ref, inverse_ref, work):
    rows = lax.broadcasted_iota(jnp.int32, (PMAX, PMAX), 0)
    columns = lax.broadcasted_iota(jnp.int32, (PMAX, PMAX), 1)
    same = (rows == columns).astype(F32)
    pivots = pivots_ref[0]
    work[:, :PMAX] = jnp.where((rows < pivots) & (columns < pivots), block_ref[...], same)
    work[:, PMAX:] = same
    small_rows = lax.broadcasted_iota(jnp.int32, (BASE, 1), 0)
    eye_rows = lax.broadcasted_iota(jnp.int32, (BASE, BASE), 0)
    eye_columns = lax.broadcasted_iota(jnp.int32, (BASE, BASE), 1)
    eye = (eye_rows == eye_columns).astype(F32)
    for step in range(PMAX // BASE):
        first = step * BASE
        last = first + BASE
        diagonal = work[first:last, first:last]
        both = jnp.concatenate([diagonal, eye, jnp.zeros((BASE, 128 - 2 * BASE), F32)], axis=1)
        for group in range(0, BASE, GROUP):
            columns_of = [jnp.broadcast_to(both[:, group + i : group + i + 1], (BASE, 128)) for i in range(GROUP)]
            rows_of = [both[group + i : group + i + 1, :] for i in range(GROUP)]
            for i in range(GROUP):
                k = group + i
                below = jnp.where(small_rows > k, columns_of[i], 0.0)
                inverse_pivot = 1.0 / columns_of[i][k : k + 1, :]
                scaled = rows_of[i] * inverse_pivot
                for j in range(i + 1, GROUP):
                    entry = columns_of[i][group + j : group + j + 1, :]
                    columns_of[j] = columns_of[j] - below * (entry * inverse_pivot)
                    rows_of[j] = rows_of[j] - entry * scaled
                both = both - below * scaled
        pivot_values = jnp.sum(both[:, :BASE] * eye, axis=1, keepdims=True)
        inverse = both[:, BASE : 2 * BASE] / jnp.sqrt(pivot_values)
        strip = exact(inverse, work[first:last, :], NN)
        work[first:last, :] = strip
        if last < PMAX:
            update = exact(strip[:, :PMAX], strip, TN)
            work[last:, :] = work[last:, :] - update[last:, :]
    inverse_ref[...] = jnp.where(rows < pivots, work[:, PMAX:], 0.0)


def inverse_factor(pivots, columns):
    return pl.pallas_call(
        cholesky_kernel,
        grid=(1,),
        out_shape=jax.ShapeDtypeStruct((PMAX, PMAX), F32),
        in_specs=[pl.BlockSpec(memory_space=pltpu.SMEM), pl.BlockSpec((PMAX, PMAX), lambda j: (0, 0))],
        out_specs=pl.BlockSpec((PMAX, PMAX), lambda j: (0, 0)),
        scratch_shapes=[pltpu.VMEM((PMAX, 2 * PMAX), F32)],
        cost_estimate=pl.CostEstimate(flops=400_000_000, bytes_accessed=524288, transcendentals=0),
        name="inverse_factor",
    )(pivots, columns)


def gather_stages(own_ref, all_ref, local_sem, send_sems, recv_sems, more=0):
    rank = lax.axis_index("grid")
    core = rank % 2
    chip = rank // 2
    x, y = chip // SIDE, chip % SIDE
    p = y + core * (x - y)
    s = x + core * (y - x)

    def device(dp, ds):
        pp, ss = (p + dp) % SIDE, (s + ds) % SIDE
        return 2 * (pp * (1 + 3 * core) + ss * (4 - 3 * core)) + core

    def rows(dp, ds, half=None):
        first = device(dp, ds) * ROWS
        if half is None:
            return pl.ds(pl.multiple_of(first, 64), ROWS)
        return pl.ds(pl.multiple_of(first + half * (ROWS // 2), 32), ROWS // 2)

    sems = (send_sems, recv_sems)
    sibling = {"grid": rank + 1 - 2 * core}
    p_up, p_down = {"grid": device(1, 0)}, {"grid": device(3, 0)}
    s_up, s_down = {"grid": device(0, 1)}, {"grid": device(0, 3)}
    greet((p_up, p_down, s_up, s_down, sibling), more)
    here = pltpu.make_async_copy(own_ref, all_ref.at[rows(0, 0)], local_sem)
    copies = []

    def send(index, where, target, source=None):
        copy = remote(all_ref.at[where] if source is None else source, all_ref.at[where], sems, index, target)
        copy.start()
        copies.append(copy)

    def arrived(index, where):
        remote(all_ref.at[where], all_ref.at[where], sems, index, sibling).wait_recv()

    def across(dp, ds, source=None):
        send(20 + 4 * dp + ds, rows(dp, ds), sibling, source)

    def sideways(dp):
        send(4 + dp, rows(dp, 0), s_up)
        send(8 + dp, rows(dp, 0), s_down)

    def begin():
        here.start()
        send(0, rows(0, 0), p_up, own_ref)
        send(1, rows(0, 0), p_down, own_ref)
        send(4, rows(0, 0), s_up, own_ref)
        send(8, rows(0, 0), s_down, own_ref)
        across(0, 0, own_ref)

    def from_below():
        arrived(0, rows(3, 0))
        send(2, rows(3, 0, 0), p_up)
        sideways(3)
        across(3, 0)

    def from_above():
        arrived(1, rows(1, 0))
        send(3, rows(1, 0, 1), p_down)
        sideways(1)
        across(1, 0)

    def pass_on(dp):
        arrived(4 + dp, rows(dp, 3))
        send(12 + dp, rows(dp, 3, 0), s_up)
        across(dp, 3)
        arrived(8 + dp, rows(dp, 1))
        send(16 + dp, rows(dp, 1, 1), s_down)
        across(dp, 1)

    def opposite():
        arrived(2, rows(2, 0, 0))
        arrived(3, rows(2, 0, 1))
        sideways(2)
        across(2, 0)

    def complete(dp):
        arrived(12 + dp, rows(dp, 2, 0))
        arrived(16 + dp, rows(dp, 2, 1))
        across(dp, 2)

    def finish():
        for copy in copies:
            copy.wait_send()
        for dp in range(SIDE):
            for ds in range(SIDE):
                chip_there = ((s + dp) % SIDE) * (4 - 3 * core) + ((p + ds) % SIDE) * (1 + 3 * core)
                first = (2 * chip_there + 1 - core) * ROWS
                arrived(20 + 4 * dp + ds, pl.ds(pl.multiple_of(first, 64), ROWS))
        here.wait()

    steps = [begin, from_below, from_above, functools.partial(pass_on, 0), opposite]
    steps += [functools.partial(pass_on, dp) for dp in (3, 1, 2)]
    steps += [functools.partial(complete, dp) for dp in (0, 3, 1, 2)]
    return steps + [finish]


def front_kernel(
    places_ref, rows_ref, own_ref, all_ref, turned_ref, both, local_sem, send_sems, recv_sems, own_sems, out_sems, in_sems
):
    rank = lax.axis_index("grid")
    core = rank % 2
    steps = gather_stages(own_ref, all_ref, local_sem, send_sems, recv_sems)
    sibling = {"grid": rank + 1 - 2 * core}
    mine = pl.ds(pl.multiple_of(core * ROWS, 64), ROWS)

    def local(j):
        lanes = pl.ds(pl.multiple_of(j * WIDE, 128), WIDE)
        return pltpu.make_async_copy(rows_ref.at[:, lanes], both.at[mine, lanes], own_sems.at[j])

    def pair(j):
        lanes = pl.ds(pl.multiple_of(j * WIDE, 128), WIDE)
        return pltpu.make_async_remote_copy(
            src_ref=rows_ref.at[:, lanes], dst_ref=both.at[mine, lanes],
            send_sem=out_sems.at[j], recv_sem=in_sems.at[j], device_id=sibling, device_id_type=MESH,
        )

    steps[0]()
    for j in range(CHIPS):
        pair(j).start()
        local(j).start()

    def here(j):
        local(j).wait()
        pair(j).wait()

    def work(j, carry):
        @pl.when(j < CHIPS - 1)
        def _():
            here(j + 1)

        first = j * WIDE + core * ROWS
        start = jnp.minimum(j * WIDE + core * 128, ORDER - 512)
        lanes = pl.ds(pl.multiple_of(start, 128), 512)
        wanted = first + lax.broadcasted_iota(jnp.int32, (ROWS, 512), 0)
        one_hot = (wanted == places_ref[:1, lanes]).astype(F32).astype(BF16)
        turned_ref[j] = pick(one_hot, both[:, lanes], NT)
        return carry

    here(0)
    done = 0
    rest = steps[1:-1]
    for index, step in enumerate(rest):
        until = (CHIPS * (index + 1)) // len(rest)
        lax.fori_loop(done, until, work, 0)
        done = until
        step()
    steps[-1]()


def front(rows, places):
    return pl.pallas_call(
        front_kernel,
        grid=(1,),
        out_shape=(
            jax.ShapeDtypeStruct((ORDER, PMAX), F32),
            jax.ShapeDtypeStruct((CHIPS, ROWS, WIDE), F32),
        ),
        in_specs=[
            pl.BlockSpec(places.shape, lambda i: (0, 0)),
            pl.BlockSpec(memory_space=pl.ANY),
            pl.BlockSpec((ROWS, PMAX), lambda i: (0, 0)),
        ],
        out_specs=(
            pl.BlockSpec((ORDER, PMAX), lambda i: (0, 0)),
            pl.BlockSpec((CHIPS, ROWS, WIDE), lambda i: (0, 0, 0)),
        ),
        scratch_shapes=[
            pltpu.VMEM((WIDE, ORDER), F32),
            pltpu.SemaphoreType.DMA,
            pltpu.SemaphoreType.DMA((36,)),
            pltpu.SemaphoreType.DMA((36,)),
            pltpu.SemaphoreType.DMA((CHIPS,)),
            pltpu.SemaphoreType.DMA((CHIPS,)),
            pltpu.SemaphoreType.DMA((CHIPS,)),
        ],
        compiler_params=pltpu.CompilerParams(collective_id=0, has_side_effects=True),
        cost_estimate=pl.CostEstimate(flops=400_000_000, bytes_accessed=25_000_000, transcendentals=0),
        name="front",
    )(places, rows, rows)


def offset_chip(chip, index, sign=1):
    dx, dy = 0, 0
    for number, (x, y) in enumerate(TURNED + SELF):
        dx = dx + jnp.where(index == number, x, 0)
        dy = dy + jnp.where(index == number, y, 0)
    return shifted(chip, (dx, dy), sign)


def post_kernel(
    weight_ref, places_ref, columns_ref, inverse_ref, moved_ref, front_ref,
    panel_ref, all_ref, sum_ref, landing_ref,
    blocks, lead, lead_landing, upper_own, z_landing, mirror, window, solved,
    local_sem, send_sems, recv_sems, z_send, z_recv, mirror_send, mirror_recv, lead_send, lead_recv,
):
    group = lax.axis_index("front")
    rank = lax.axis_index("grid")
    core = rank % 2
    chip = rank // 2
    turned = len(TURNED)
    total = turned + len(SELF)
    up, down = {"front": (group + 1) % SIDE}, {"front": (group + 3) % SIDE}
    others = [{"front": (group + d) % SIDE} for d in range(1, SIDE)]

    def mirror_device(index, k, sign):
        return {"grid": 2 * offset_chip(chip, index, sign) + k}

    barrier = pltpu.get_barrier_semaphore()
    for device in others:
        pl.semaphore_signal(barrier, inc=1, device_id=device, device_id_type=MESH)
    for index in range(turned):
        for k in range(2):
            pl.semaphore_signal(barrier, inc=1, device_id=mirror_device(index, k, -1), device_id_type=MESH)
    steps = gather_stages(upper_own, all_ref, local_sem, send_sems, recv_sems, len(others) + 2 * turned)

    inverse = inverse_ref[...]
    panel_ref[...] = exact(columns_ref[pl.ds(pl.multiple_of(rank * ROWS, 64), ROWS), :], inverse, NT)
    after = jnp.minimum(chip + 1, CHIPS - 1)

    def piece(index):
        return columns_ref[pl.ds(pl.multiple_of(index * WIDE, 128), WIDE), :]

    def places_at(index):
        return places_ref[:1, pl.ds(pl.multiple_of(index * WIDE, 128), WIDE)]

    wanted_rows = rank * ROWS + lax.broadcasted_iota(jnp.int32, (ROWS, WIDE), 0)
    picked = pick((wanted_rows == places_at(chip)).astype(F32).astype(BF16), piece(chip), NN)
    picked += pick((wanted_rows == places_at(chip + 1)).astype(F32).astype(BF16), piece(after), NN)
    solved[...] = exact(exact(picked, inverse, NT), inverse, NN)

    def block(where):
        following = jnp.minimum(where + 1, CHIPS - 1)
        w = solved[...]
        window[:, :WIDE] = moved_ref[where] - product(w, piece(where), NT)
        window[:, WIDE:] = moved_ref[following] - product(w, piece(following), NT)
        first = where * WIDE

        def part(low, wide):
            wanted = first + low + lax.broadcasted_iota(jnp.int32, (wide, wide + 256), 0)
            lanes = pl.ds(pl.multiple_of(first + low, 128), wide + 256)
            one_hot = (wanted == places_ref[:1, lanes]).astype(F32).astype(BF16)
            high, rest = split(window[:, low : low + wide + 256])
            return dot(high, one_hot, NT) + dot(rest, one_hot, NT)

        return jnp.concatenate([part(0, 256), part(256, 128)], axis=1)

    z_sems = (z_send, z_recv)
    upper, lower = pl.ds(0, ROWS // 2), pl.ds(ROWS // 2, ROWS // 2)

    def z_copy(index, which):
        if which == 0:
            return remote(blocks.at[index], z_landing.at[0, index], z_sems, 4 * index, up)
        if which == 1:
            return remote(blocks.at[index], z_landing.at[2, index], z_sems, 4 * index + 1, down)
        if which == 2:
            return remote(z_landing.at[0, index, upper], z_landing.at[1, index, upper], z_sems, 4 * index + 2, up)
        return remote(z_landing.at[2, index, lower], z_landing.at[1, index, lower], z_sems, 4 * index + 3, down)

    def z_begin(index):
        z_copy(index, 0).start()
        z_copy(index, 1).start()

    def z_forward(index):
        z_copy(index, 0).wait_recv()
        z_copy(index, 2).start()
        z_copy(index, 1).wait_recv()
        z_copy(index, 3).start()

    def z_sum(index):
        z_copy(index, 2).wait_recv()
        z_copy(index, 3).wait_recv()
        result = weight_ref[0] * blocks[index]
        for d in range(SIDE - 1):
            result = result + weight_ref[d + 1] * z_landing[d, index]
        sum_ref[index] = result
        return result

    def lead_copy(d):
        return remote(lead.at[:, pl.ds(0, LEAD)], lead_landing.at[d], (lead_send, lead_recv), d, others[d])

    def mirror_copy(index, k, arriving=False):
        slot = k if arriving else core
        return pltpu.make_async_remote_copy(
            src_ref=mirror.at[index, k], dst_ref=landing_ref.at[index, slot],
            send_sem=mirror_send.at[2 * index + k], recv_sem=mirror_recv.at[2 * index + slot],
            device_id=mirror_device(index, k, 1), device_id_type=MESH,
        )

    def fold(index, carry):
        turned_block = z_sum(index).T

        @pl.when(index > 0)
        def _():
            for k in range(2):
                mirror_copy(index - 1, k).start()

        mirror[index, 0] = turned_block[:ROWS]
        mirror[index, 1] = turned_block[ROWS:]
        return carry

    lead[...] = block(0 * chip)

    def compute(index, carry):
        result = block(offset_chip(chip, index))

        @pl.when(index == 0)
        def _():
            for d in range(SIDE - 1):
                lead_copy(d).start()

        @pl.when((index > 0) & (index <= turned))
        def _():
            z_begin(index - 1)

        blocks[index] = result
        return carry

    lax.fori_loop(0, total, compute, 0)
    leading = front_ref[...] + weight_ref[0] * lead[:, :LEAD]
    for d in range(SIDE - 1):
        lead_copy(d).wait()
        leading = leading + weight_ref[d + 1] * lead_landing[d]
    upper_own[...] = leading
    z_forward(0)
    steps[0]()
    z_forward(1)
    steps[1]()
    steps[2]()
    z_forward(2)
    steps[3]()
    steps[4]()
    z_forward(3)
    steps[5]()
    steps[6]()
    z_forward(4)
    steps[7]()
    z_forward(5)

    def z_rest(index, carry):
        z_begin(index)
        return carry

    lax.fori_loop(turned, total, z_rest, 0)
    for step in steps[8:]:
        step()
    lax.fori_loop(0, turned, fold, 0)

    def forward(index, carry):
        z_forward(index)
        return carry

    lax.fori_loop(turned, turned + 1, forward, 0)
    for k in range(2):
        mirror_copy(turned - 1, k).start()
    lax.fori_loop(turned + 1, total, forward, 0)

    def own_sum(index, carry):
        z_sum(index)
        return carry

    lax.fori_loop(turned, total, own_sum, 0)

    def drain(index, carry):
        for which in range(4):
            z_copy(index, which).wait_send()
        return carry

    lax.fori_loop(0, total, drain, 0)

    def settle(index, carry):
        for k in range(2):
            mirror_copy(index, k).wait_send()
            mirror_copy(index, k, True).wait_recv()
        return carry

    lax.fori_loop(0, turned, settle, 0)


def post(weights, places, columns, inverse, moved, front):
    turned = len(TURNED)
    total = turned + len(SELF)
    dma = pltpu.SemaphoreType.DMA
    whole = lambda shape: pl.BlockSpec(shape, lambda i: (0,) * len(shape))
    outs = [(ROWS, PMAX), (ORDER, PMAX), (total, ROWS, WIDE), (turned, 2, ROWS, ROWS)]
    return pl.pallas_call(
        post_kernel,
        grid=(1,),
        out_shape=tuple(jax.ShapeDtypeStruct(shape, F32) for shape in outs),
        in_specs=[
            pl.BlockSpec(memory_space=pltpu.SMEM),
            whole(places.shape),
            whole((ORDER, PMAX)),
            whole((PMAX, PMAX)),
            whole((CHIPS, ROWS, WIDE)),
            pl.BlockSpec((ROWS, LEAD), lambda i: (0, 0)),
        ],
        out_specs=tuple(whole(shape) for shape in outs),
        scratch_shapes=[
            pltpu.VMEM((total, ROWS, WIDE), F32),
            pltpu.VMEM((ROWS, WIDE), F32),
            pltpu.VMEM((SIDE - 1, ROWS, LEAD), F32),
            pltpu.VMEM((ROWS, LEAD), F32),
            pltpu.VMEM((SIDE - 1, total, ROWS, WIDE), F32),
            pltpu.VMEM((turned, 2, ROWS, ROWS), F32),
            pltpu.VMEM((ROWS, 2 * WIDE), F32),
            pltpu.VMEM((ROWS, PMAX), F32),
            dma,
            dma((36,)),
            dma((36,)),
            dma((4 * total,)),
            dma((4 * total,)),
            dma((2 * turned,)),
            dma((2 * turned,)),
            dma((SIDE - 1,)),
            dma((SIDE - 1,)),
        ],
        compiler_params=pltpu.CompilerParams(collective_id=1, has_side_effects=True),
        cost_estimate=pl.CostEstimate(flops=400_000_000, bytes_accessed=25_000_000, transcendentals=0),
        name="post",
    )(weights, places, columns, inverse, moved, front)


def parent_kernel(
    order_ref, pivots_ref, own_ref, here_ref, inverse_ref, sum_ref, mirror_ref, front_ref, panel_ref, schur_ref, weights
):
    step = pl.program_id(0)
    grid_rank = lax.axis_index("grid")
    sums = len(TURNED) + len(SELF)

    @pl.when(step == 0)
    def _():
        inverse = inverse_ref[...]
        panel = exact(own_ref[...], inverse, NT)
        panel_ref[...] = panel
        weights[...] = exact(panel, inverse, NN)

    total = front_ref[...] - product(here_ref[...], weights[...], NT).T
    pivots = pivots_ref[0]
    rows = grid_rank * ROWS + lax.broadcasted_iota(jnp.int32, (ROWS, WIDE), 0)
    columns = order_ref[step] * WIDE + lax.broadcasted_iota(jnp.int32, (ROWS, WIDE), 1)
    keep = (rows >= pivots) & (columns >= pivots)

    @pl.when(step < sums)
    def _():
        schur_ref[...] = jnp.where(keep, total + sum_ref[0], 0.0)

    @pl.when(step >= sums)
    def _():
        mirror = jnp.concatenate([mirror_ref[0, 0], mirror_ref[0, 1]], axis=1)
        schur_ref[...] = jnp.where(keep, total + mirror, 0.0)


def parent_schur(order, pivots, columns, inverse, sums, mirror, front):
    count = len(TURNED) + len(SELF)
    spec = pltpu.PrefetchScalarGridSpec(
        num_scalar_prefetch=1,
        grid=(CHIPS,),
        in_specs=[
            pl.BlockSpec(memory_space=pltpu.SMEM),
            pl.BlockSpec((ROWS, PMAX), lambda i, order: (order[CHIPS], 0)),
            pl.BlockSpec((WIDE, PMAX), lambda i, order: (order[i], 0)),
            pl.BlockSpec((PMAX, PMAX), lambda i, order: (0, 0)),
            pl.BlockSpec((1, ROWS, WIDE), lambda i, order: (jnp.minimum(i, count - 1), 0, 0)),
            pl.BlockSpec((1, 2, ROWS, ROWS), lambda i, order: (jnp.maximum(i - count, 0), 0, 0, 0)),
            pl.BlockSpec((ROWS, WIDE), lambda i, order: (0, order[i])),
        ],
        out_specs=(
            pl.BlockSpec((ROWS, PMAX), lambda i, order: (0, 0)),
            pl.BlockSpec((ROWS, WIDE), lambda i, order: (0, order[i])),
        ),
        scratch_shapes=[pltpu.VMEM((ROWS, PMAX), F32)],
    )
    return pl.pallas_call(
        parent_kernel,
        grid_spec=spec,
        out_shape=(jax.ShapeDtypeStruct((ROWS, PMAX), F32), jax.ShapeDtypeStruct((ROWS, ORDER), F32)),
        cost_estimate=pl.CostEstimate(flops=400_000_000, bytes_accessed=30_000_000, transcendentals=0),
        name="parent_schur",
    )(order, pivots, columns, columns, inverse, sums, mirror, front)


def on_device(child_fronts, parent_fronts, child_maps, parent_of, child_pivots, parent_pivots):
    front_group = lax.axis_index("front")
    rank = lax.axis_index("grid")
    chip = rank // 2
    front_rows = child_fronts[0]
    pivots = lax.dynamic_slice(child_pivots, (front_group,), (1,))
    upper_pivots = lax.dynamic_slice(parent_pivots, (front_group,), (1,))
    groups = (front_group - jnp.arange(SIDE, dtype=jnp.int32)) % SIDE
    weights = (parent_of[groups] == front_group).astype(F32)
    number = jnp.arange(CHIPS + 1, dtype=jnp.int32)
    count = len(TURNED) + len(SELF)
    sign = jnp.where(number < count, 1, -1)
    order = offset_chip(chip, jnp.where(number < count, number, number - count), sign)
    order = jnp.where(number < CHIPS, order, rank)

    position = jnp.arange(ORDER, dtype=jnp.int32)
    line = jnp.where(position >= pivots, child_maps[front_group], -1)
    line = jnp.pad(line, (0, 2 * WIDE), constant_values=-1)
    places = jnp.broadcast_to(line[None], (8, line.shape[0]))
    columns, turned = front(front_rows, places)
    same_core = [[2 * c + k for c in range(CHIPS)] for k in range(2)]
    moved = lax.all_to_all(turned, "grid", 0, 0, axis_index_groups=same_core)
    inverse = inverse_factor(pivots, columns)
    panel_rows, upper_columns, sums, mirror = post(weights, places, columns, inverse, moved, parent_fronts[0])
    upper_inverse = inverse_factor(upper_pivots, upper_columns)
    upper_panel, upper_schur = parent_schur(
        order, upper_pivots, upper_columns, upper_inverse, sums, mirror, parent_fronts[0]
    )
    return (panel_rows[None], upper_panel[None], upper_schur[None])


def solution(mesh):
    in_specs = (P("front", "grid", None), P("front", "grid", None), P(), P(), P(), P())
    out_specs = (P("front", "grid", None), P("front", "grid", None), P("front", "grid", None))
    return jax.shard_map(
        on_device, mesh=mesh, in_specs=in_specs, out_specs=out_specs, check_vma=False
    )
```

time: 295 us -> 276 us (0.936)
  waiting for transfers between devices: 63.4 us -> 47.1 us
  between operations: 14.4 us -> 0.77 us
  Pallas kernels: 203 us -> 215 us
    all_gather x2 -> x0, waiting for transfers between devices: 14.4 us -> none  [the longest x1 7.71 us: on_device(): turned_all = lax.all_gather(turned_part, 'front', axis=0)]
    pallas_call x5 -> x1, Pallas kernels: 121 us -> 134 us  [post(): pl.pallas_call(post_kernel, grid=(1,), out_shape=tuple((jax.ShapeDtypeStr...]
  transfers between devices with their start and end apart: 3 -> 1, of which waited for: 3 -> 1; matrix products, arithmetic and copies ran while one was open for 1% -> 1% of each run, Pallas kernels for 46% -> 6%
where the time goes in v4:
time: 276 us; the launch traced here: 274 us
  Pallas kernels  215 us (78%)
  waiting for transfers between devices  47.1 us (17%)
  starting transfers between devices  5.65 us (2%)
  local copies, waits for them, and re-layouts  3.99 us (1%)
    pallas_call x1, Pallas kernels, post(): pl.pallas_call(post_kernel, grid=(1,), out_shape=tuple((jax.ShapeDtypeStr...  134 us
    all_to_all x1, waiting for transfers between devices, on_device(): moved = lax.all_to_all(turned, 'grid', 0, 0, axis_index_groups=same_core)  47.1 us
    pallas_call x1, Pallas kernels, front(): pl.pallas_call(front_kernel, grid=(1,), out_shape=(jax.ShapeDtypeStruct((...  31.6 us
    pallas_call x2, Pallas kernels, inverse_factor(): pl.pallas_call(cholesky_kernel, grid=(1,), out_shape=jax.ShapeDtypeStruct...  30.3 us
    pallas_call x1, Pallas kernels, parent_schur(): pl.pallas_call(parent_kernel, grid_spec=spec, out_shape=(jax.ShapeDtypeSt...  18.8 us
    all_to_all x1, starting transfers between devices, on_device(): moved = lax.all_to_all(turned, 'grid', 0, 0, axis_index_groups=same_core)  5.65 us
  transfers between devices with their start and end apart: 1, of which 1 were waited for; matrix products, arithmetic and copies ran while one was open for 1% of the time, Pallas kernels for 6%

profile of v4, /device:TPU:0, one launch (start us, length us, event | category | flops | bytes accessed | tf_op | source)
XLA Modules:
  0.0 274.4 jit_solution(2847496239203719895)
XLA Ops:
  0.6 0.0 copy-start
  0.7 1.3 dynamic_slice.9.pivots_ref
  1.9 0.0 copy-done
  2.0 0.7 fusion
  2.6 0.7 broadcast_in_dim.75.places_ref
  3.3 31.6 %front.1 = (f32[6144,256]{1,0:T(8,128)}, f32[16,192,384]{2,1,0:T(8,128)}) custom-call(s32[8,6912]{1,0:T(8,128)} %broadcast_in_dim.75.places_ref, f32[192,6144]{1,0:T(8,128)} %bitcast.11, f32[192,6144]{1,0:T(8,128)} %bitcast.12), custom_call_target="tpu_custom_call" | custom-call | flops 400000000 | bytes 25000000 | tf_op jit(solution)/shard_map/front/pallas_call | solution.py:277
  35.0 0.0 copy-start.3
  35.0 0.0 copy-start.1
  35.0 5.6 %all-to-all-start = ((f32[16,192,384]{2,1,0:T(8,128)}), f32[16,192,384]{2,1,0:T(8,128)}, u32[]{:S(2)}, u32[]{:S(2)}) async-start(f32[16,192,384]{2,1,0:T(8,128)} %get-tuple-element.12), calls=%async_computation | async-start | bytes 9437184 | tf_op jit(solution)/shard_map/all_to_all | solution.py:629
  40.7 0.0 copy-done.3
  40.7 0.7 dynamic_slice.11.pivots_ref
  41.4 0.0 copy-done.1
  41.4 0.6 gather_fusion
  42.0 15.1 %inverse_factor.2.inverse_ref = f32[256,256]{1,0:T(8,128)} custom-call(s32[1]{0:T(128)} %dynamic_slice.9.pivots_ref, f32[6144,256]{1,0:T(8,128)} %get-tuple-element.11.block_ref.columns_ref), custom_call_target="tpu_custom_call" | custom-call | flops 400000000 | bytes 524288 | tf_op jit(solution)/shard_map/inverse_factor/pallas_call | solution.py:115
  57.2 0.5 compare_select_fusion.15.order_ref
  57.7 0.5 compare_convert_fusion.weight_ref
  58.2 47.1 %all-to-all-done.moved_ref = f32[16,192,384]{2,1,0:T(8,128)} async-done(((f32[16,192,384]{2,1,0:T(8,128)}), f32[16,192,384]{2,1,0:T(8,128)}, u32[]{:S(2)}, u32[]{:S(2)}) %all-to-all-start) | async-done | bytes 4718624 | tf_op jit(solution)/shard_map/all_to_all | solution.py:629
  105.3 134.5 %post.1 = (f32[192,256]{1,0:T(8,128)}, f32[6144,256]{1,0:T(8,128)}, f32[10,192,384]{2,1,0:T(8,128)}, f32[6,2,192,192]{3,2,1,0:T(8,128)}) custom-call(f32[4]{0:T(128)} %compare_convert_fusion.weight_ref, s32[8,6912]{1,0:T(8,128)} %broadcast_in_dim.75.places_ref, f32[6144,256]{1,0:T(8,128)} %get-tuple-element.11.block_ref.columns_ref, ...), custom_call_target="tpu_custom_call" | custom-call | flops 400000000 | bytes 25000000 | tf_op jit(solution)/shard_map/post/pallas_call | solution.py:511
  239.8 15.1 %inverse_factor.3.inverse_ref = f32[256,256]{1,0:T(8,128)} custom-call(s32[1]{0:T(128)} %dynamic_slice.11.pivots_ref, f32[6144,256]{1,0:T(8,128)} %get-tuple-element.14.block_ref.own_ref.here_ref), custom_call_target="tpu_custom_call" | custom-call | flops 400000000 | bytes 524288 | tf_op jit(solution)/shard_map/inverse_factor/pallas_call | solution.py:115
  254.9 0.0 copy-start.2
  254.9 18.8 %parent_schur.1 = (f32[192,256]{1,0:T(8,128)}, f32[192,6144]{1,0:T(8,128)}) custom-call(s32[17]{0:T(128)} %compare_select_fusion.15.order_ref, s32[1]{0:T(128)} %dynamic_slice.11.pivots_ref, f32[6144,256]{1,0:T(8,128)} %get-tuple-element.14.block_ref.own_ref.here_ref, f32[6144,256]{1,0:T(8,128)} %get-tuple-element.14.block_ref.own_ref.here_ref, ...), custom_call_target="tpu_custom_call" | custom-call | flops 400000000 | bytes 30000000 | tf_op jit(solution)/shard_map/parent_schur/pallas_call | solution.py:599
  273.7 0.0 copy-done.2
  273.7 0.7 copy.10
  (4 shorter events, 0.0 us)
Async XLA Ops:
  0.6 1.3 copy-start
  35.0 5.7 %copy-start.3 = (s32[4]{0:T(128)S(1)}, s32[4]{0:T(128)}, u32[]{:S(2)}) copy-start(s32[4]{0:T(128)} %param.11) | copy-start | bytes 52
  35.0 6.4 %copy-start.1 = (s32[4]{0:T(128)S(1)}, s32[4]{0:T(128)}, u32[]{:S(2)}) copy-start(s32[4]{0:T(128)} %param.9) | copy-start | bytes 52
  35.0 70.3 %all-to-all-start = ((f32[16,192,384]{2,1,0:T(8,128)}), f32[16,192,384]{2,1,0:T(8,128)}, u32[]{:S(2)}, u32[]{:S(2)}) async-start(f32[16,192,384]{2,1,0:T(8,128)} %get-tuple-element.12), calls=%async_computation | async-start | bytes 9437184 | tf_op jit(solution)/shard_map/all_to_all | solution.py:629
  254.9 18.8 %copy-start.2 = (f32[192,256]{1,0:T(8,128)S(1)}, f32[192,256]{1,0:T(8,128)}, u32[]{:S(2)}) copy-start(f32[192,256]{1,0:T(8,128)} %get-tuple-element.13) | copy-start | bytes 589828

commit v5 on v4

--- a/solution.py
+++ b/solution.py
@@ -13,6 +13,7 @@
 ROWS = 192
 WIDE = 384
 ORDER = 6144
+HALF = 96
 BASE = 32
 GROUP = 8
 LEAD = 256
@@ -40,7 +41,8 @@
 def product(a, b, dims):
     a_high, a_low = split(a)
     b_high, b_low = split(b)
-    return dot(a_high, b_high, dims) + (dot(a_high, b_low, dims) + dot(a_low, b_high, dims))
+    both = dot(jnp.concatenate([a_high, a_low], axis=0), b_high, dims)
+    return both[: a.shape[0]] + (both[a.shape[0] :] + dot(a_high, b_low, dims))
 
 
 def pick(one_hot, a, dims):
@@ -72,22 +74,26 @@
     pl.semaphore_wait(barrier, len(devices) + more)
 
 
-def cholesky_kernel(pivots_ref, block_ref, inverse_ref, work):
+def factor_into(pivots, block, inverse_ref, work):
     rows = lax.broadcasted_iota(jnp.int32, (PMAX, PMAX), 0)
     columns = lax.broadcasted_iota(jnp.int32, (PMAX, PMAX), 1)
     same = (rows == columns).astype(F32)
-    pivots = pivots_ref[0]
-    work[:, :PMAX] = jnp.where((rows < pivots) & (columns < pivots), block_ref[...], same)
+    work[:, :PMAX] = jnp.where((rows < pivots) & (columns < pivots), block, same)
     work[:, PMAX:] = same
     small_rows = lax.broadcasted_iota(jnp.int32, (BASE, 1), 0)
-    eye_rows = lax.broadcasted_iota(jnp.int32, (BASE, BASE), 0)
-    eye_columns = lax.broadcasted_iota(jnp.int32, (BASE, BASE), 1)
+    eye_rows = lax.broadcasted_iota(jnp.int32, (BASE, 128), 0)
+    eye_columns = lax.broadcasted_iota(jnp.int32, (BASE, 128), 1)
     eye = (eye_rows == eye_columns).astype(F32)
-    for step in range(PMAX // BASE):
-        first = step * BASE
-        last = first + BASE
-        diagonal = work[first:last, first:last]
-        both = jnp.concatenate([diagonal, eye, jnp.zeros((BASE, 128 - 2 * BASE), F32)], axis=1)
+    eye_after = (eye_rows + BASE == eye_columns).astype(F32)
+    all_rows = lax.broadcasted_iota(jnp.int32, (PMAX, 1), 0)
+    tall_rows = lax.broadcasted_iota(jnp.int32, (PMAX, 128), 0)
+    tall_columns = lax.broadcasted_iota(jnp.int32, (PMAX, 128), 1)
+
+    def step(index, carry):
+        first = index * BASE
+        here = pl.ds(pl.multiple_of(first, BASE), BASE)
+        chosen = ((tall_rows == tall_columns + first) & (tall_columns < BASE)).astype(F32)
+        both = exact(work[here, :PMAX], chosen, NN) + eye_after
         for group in range(0, BASE, GROUP):
             columns_of = [jnp.broadcast_to(both[:, group + i : group + i + 1], (BASE, 128)) for i in range(GROUP)]
             rows_of = [both[group + i : group + i + 1, :] for i in range(GROUP)]
@@ -101,14 +107,20 @@
                     columns_of[j] = columns_of[j] - below * (entry * inverse_pivot)
                     rows_of[j] = rows_of[j] - entry * scaled
                 both = both - below * scaled
-        pivot_values = jnp.sum(both[:, :BASE] * eye, axis=1, keepdims=True)
+        pivot_values = jnp.sum(both * eye, axis=1, keepdims=True)
         inverse = both[:, BASE : 2 * BASE] / jnp.sqrt(pivot_values)
-        strip = exact(inverse, work[first:last, :], NN)
-        work[first:last, :] = strip
-        if last < PMAX:
-            update = exact(strip[:, :PMAX], strip, TN)
-            work[last:, :] = work[last:, :] - update[last:, :]
+        strip = exact(inverse, work[here, :], NN)
+        update = exact(strip[:, :PMAX], strip, TN)
+        work[...] = work[...] - jnp.where(all_rows >= first + BASE, update, 0.0)
+        work[here, :] = strip
+        return carry
+
+    lax.fori_loop(0, PMAX // BASE, step, 0)
     inverse_ref[...] = jnp.where(rows < pivots, work[:, PMAX:], 0.0)
+
+
+def cholesky_kernel(pivots_ref, block_ref, inverse_ref, work):
+    factor_into(pivots_ref[0], block_ref[...], inverse_ref, work)
 
 
 def inverse_factor(pivots, columns):
@@ -221,7 +233,7 @@
 
 
 def front_kernel(
-    places_ref, rows_ref, own_ref, all_ref, turned_ref, both, local_sem, send_sems, recv_sems, own_sems, out_sems, in_sems
+    places_ref, rows_ref, own_ref, all_ref, turned_ref, later_ref, both, local_sem, send_sems, recv_sems, own_sems, out_sems, in_sems
 ):
     rank = lax.axis_index("grid")
     core = rank % 2
@@ -259,7 +271,9 @@
         lanes = pl.ds(pl.multiple_of(start, 128), 512)
         wanted = first + lax.broadcasted_iota(jnp.int32, (ROWS, 512), 0)
         one_hot = (wanted == places_ref[:1, lanes]).astype(F32).astype(BF16)
-        turned_ref[j] = pick(one_hot, both[:, lanes], NT)
+        result = pick(one_hot, both[:, lanes], NT)
+        turned_ref[j] = result[:HALF]
+        later_ref[j] = result[HALF:]
         return carry
 
     here(0)
@@ -279,7 +293,8 @@
         grid=(1,),
         out_shape=(
             jax.ShapeDtypeStruct((ORDER, PMAX), F32),
-            jax.ShapeDtypeStruct((CHIPS, ROWS, WIDE), F32),
+            jax.ShapeDtypeStruct((CHIPS, HALF, WIDE), F32),
+            jax.ShapeDtypeStruct((CHIPS, HALF, WIDE), F32),
         ),
         in_specs=[
             pl.BlockSpec(places.shape, lambda i: (0, 0)),
@@ -288,7 +303,8 @@
         ],
         out_specs=(
             pl.BlockSpec((ORDER, PMAX), lambda i: (0, 0)),
-            pl.BlockSpec((CHIPS, ROWS, WIDE), lambda i: (0, 0, 0)),
+            pl.BlockSpec((CHIPS, HALF, WIDE), lambda i: (0, 0, 0)),
+            pl.BlockSpec((CHIPS, HALF, WIDE), lambda i: (0, 0, 0)),
         ),
         scratch_shapes=[
             pltpu.VMEM((WIDE, ORDER), F32),
@@ -313,11 +329,18 @@
     return shifted(chip, (dx, dy), sign)
 
 
+LEAVING = (
+    (0, 1), (1, 0), (0, 3), (3, 0), (1, 1), (3, 3), (1, 3), (3, 1),
+    (0, 2), (2, 0), (1, 2), (2, 1), (3, 2), (2, 3), (2, 2),
+)
+
+
 def post_kernel(
-    weight_ref, places_ref, columns_ref, inverse_ref, moved_ref, front_ref,
-    panel_ref, all_ref, sum_ref, landing_ref,
-    blocks, lead, lead_landing, upper_own, z_landing, mirror, window, solved,
+    weight_ref, pivots_ref, places_ref, columns_ref, inverse_ref, moved_ref, later_ref, front_ref,
+    panel_ref, all_ref, upper_inverse_ref, sum_ref, landing_ref,
+    moved_later, blocks, lead, lead_landing, upper_own, z_landing, mirror, window, solved, work,
     local_sem, send_sems, recv_sems, z_send, z_recv, mirror_send, mirror_recv, lead_send, lead_recv,
+    later_send, later_recv, later_local,
 ):
     group = lax.axis_index("front")
     rank = lax.axis_index("grid")
@@ -337,7 +360,22 @@
     for index in range(turned):
         for k in range(2):
             pl.semaphore_signal(barrier, inc=1, device_id=mirror_device(index, k, -1), device_id_type=MESH)
-    steps = gather_stages(upper_own, all_ref, local_sem, send_sems, recv_sems, len(others) + 2 * turned)
+    for offset in LEAVING:
+        device = {"grid": 2 * shifted(chip, offset) + core}
+        pl.semaphore_signal(barrier, inc=1, device_id=device, device_id_type=MESH)
+    more = len(others) + 2 * turned + len(LEAVING)
+    steps = gather_stages(upper_own, all_ref, local_sem, send_sems, recv_sems, more)
+
+    kept = pltpu.make_async_copy(later_ref.at[chip], moved_later.at[chip], later_local)
+    kept.start()
+    leaving = []
+    for number, offset in enumerate(LEAVING):
+        to = shifted(chip, offset, -1)
+        copy = remote(
+            later_ref.at[to], moved_later.at[chip], (later_send, later_recv), number, {"grid": 2 * to + core}
+        )
+        copy.start()
+        leaving.append(copy)
 
     inverse = inverse_ref[...]
     panel_ref[...] = exact(columns_ref[pl.ds(pl.multiple_of(rank * ROWS, 64), ROWS), :], inverse, NT)
@@ -354,196 +392,217 @@
     picked += pick((wanted_rows == places_at(chip + 1)).astype(F32).astype(BF16), piece(after), NN)
     solved[...] = exact(exact(picked, inverse, NT), inverse, NN)
 
-    def block(where):
+    def block(where, half):
+        source = moved_later if half else moved_ref
         following = jnp.minimum(where + 1, CHIPS - 1)
-        w = solved[...]
-        window[:, :WIDE] = moved_ref[where] - product(w, piece(where), NT)
-        window[:, WIDE:] = moved_ref[following] - product(w, piece(following), NT)
+        w = solved[half * HALF : (half + 1) * HALF, :]
+        window[:, :WIDE] = source[where] - product(piece(where), w, NT).T
+        window[:, WIDE:] = source[following] - product(piece(following), w, NT).T
         first = where * WIDE
 
         def part(low, wide):
             wanted = first + low + lax.broadcasted_iota(jnp.int32, (wide, wide + 256), 0)
             lanes = pl.ds(pl.multiple_of(first + low, 128), wide + 256)
             one_hot = (wanted == places_ref[:1, lanes]).astype(F32).astype(BF16)
-            high, rest = split(window[:, low : low + wide + 256])
-            return dot(high, one_hot, NT) + dot(rest, one_hot, NT)
+            both = dot(jnp.concatenate(split(window[:, low : low + wide + 256]), axis=0), one_hot, NT)
+            return both[:HALF] + both[HALF:]
 
         return jnp.concatenate([part(0, 256), part(256, 128)], axis=1)
 
     z_sems = (z_send, z_recv)
-    upper, lower = pl.ds(0, ROWS // 2), pl.ds(ROWS // 2, ROWS // 2)
-
-    def z_copy(index, which):
+
+    def z_copy(index, half, which):
+        sem = 4 * (2 * index + half) + which
+        every = pl.ds(half * HALF, HALF)
+        upper = pl.ds(half * HALF, HALF // 2)
+        lower = pl.ds(half * HALF + HALF // 2, HALF // 2)
         if which == 0:
-            return remote(blocks.at[index], z_landing.at[0, index], z_sems, 4 * index, up)
+            return remote(blocks.at[index, every], z_landing.at[0, index, every], z_sems, sem, up)
         if which == 1:
-            return remote(blocks.at[index], z_landing.at[2, index], z_sems, 4 * index + 1, down)
+            return remote(blocks.at[index, every], z_landing.at[2, index, every], z_sems, sem, down)
         if which == 2:
-            return remote(z_landing.at[0, index, upper], z_landing.at[1, index, upper], z_sems, 4 * index + 2, up)
-        return remote(z_landing.at[2, index, lower], z_landing.at[1, index, lower], z_sems, 4 * index + 3, down)
-
-    def z_begin(index):
-        z_copy(index, 0).start()
-        z_copy(index, 1).start()
-
-    def z_forward(index):
-        z_copy(index, 0).wait_recv()
-        z_copy(index, 2).start()
-        z_copy(index, 1).wait_recv()
-        z_copy(index, 3).start()
-
-    def z_sum(index):
-        z_copy(index, 2).wait_recv()
-        z_copy(index, 3).wait_recv()
-        result = weight_ref[0] * blocks[index]
+            return remote(z_landing.at[0, index, upper], z_landing.at[1, index, upper], z_sems, sem, up)
+        return remote(z_landing.at[2, index, lower], z_landing.at[1, index, lower], z_sems, sem, down)
+
+    def z_begin(index, half):
+        z_copy(index, half, 0).start()
+        z_copy(index, half, 1).start()
+
+    def z_forward(index, half):
+        z_copy(index, half, 0).wait_recv()
+        z_copy(index, half, 2).start()
+        z_copy(index, half, 1).wait_recv()
+        z_copy(index, half, 3).start()
+
+    def z_sum(index, half):
+        z_copy(index, half, 2).wait_recv()
+        z_copy(index, half, 3).wait_recv()
+        every = pl.ds(half * HALF, HALF)
+        result = weight_ref[0] * blocks[index, every]
         for d in range(SIDE - 1):
-            result = result + weight_ref[d + 1] * z_landing[d, index]
-        sum_ref[index] = result
+            result = result + weight_ref[d + 1] * z_landing[d, index, every]
+        sum_ref[index, every] = result
         return result
 
     def lead_copy(d):
         return remote(lead.at[:, pl.ds(0, LEAD)], lead_landing.at[d], (lead_send, lead_recv), d, others[d])
 
-    def mirror_copy(index, k, arriving=False):
+    def mirror_copy(index, half, k, arriving=False):
         slot = k if arriving else core
         return pltpu.make_async_remote_copy(
-            src_ref=mirror.at[index, k], dst_ref=landing_ref.at[index, slot],
-            send_sem=mirror_send.at[2 * index + k], recv_sem=mirror_recv.at[2 * index + slot],
+            src_ref=mirror.at[index, half, k], dst_ref=landing_ref.at[index, slot, half],
+            send_sem=mirror_send.at[4 * index + 2 * half + k],
+            recv_sem=mirror_recv.at[4 * index + 2 * half + slot],
             device_id=mirror_device(index, k, 1), device_id_type=MESH,
         )
 
-    def fold(index, carry):
-        turned_block = z_sum(index).T
-
-        @pl.when(index > 0)
-        def _():
-            for k in range(2):
-                mirror_copy(index - 1, k).start()
-
-        mirror[index, 0] = turned_block[:ROWS]
-        mirror[index, 1] = turned_block[ROWS:]
-        return carry
-
-    lead[...] = block(0 * chip)
-
-    def compute(index, carry):
-        result = block(offset_chip(chip, index))
-
-        @pl.when(index == 0)
-        def _():
-            for d in range(SIDE - 1):
-                lead_copy(d).start()
-
-        @pl.when((index > 0) & (index <= turned))
-        def _():
-            z_begin(index - 1)
-
-        blocks[index] = result
-        return carry
-
-    lax.fori_loop(0, total, compute, 0)
+    def mirror_begin(index, half):
+        for k in range(2):
+            mirror_copy(index, half, k).start()
+
+    def each(first, last, work):
+        def body(index, carry):
+            work(index)
+            return carry
+
+        lax.fori_loop(first, last, body, 0)
+
+    def fold(half):
+        def work(index):
+            turned_block = z_sum(index, half).T
+
+            @pl.when(index > 0)
+            def _():
+                mirror_begin(index - 1, half)
+
+            mirror[index, half, 0] = turned_block[:ROWS]
+            mirror[index, half, 1] = turned_block[ROWS:]
+
+        return work
+
+    def compute(half):
+        def work(index):
+            result = block(offset_chip(chip, index), half)
+
+            @pl.when((index > 0) & (index <= turned))
+            def _():
+                z_begin(index - 1, half)
+
+            blocks[index, half * HALF : (half + 1) * HALF] = result
+
+        return work
+
+    lead[:HALF] = block(0 * chip, 0)
+    each(0, total, compute(0))
+    each(0, turned, lambda index: z_forward(index, 0))
+    each(turned, total, lambda index: z_begin(index, 0))
+    each(0, turned, fold(0))
+    for copy in leaving:
+        copy.wait()
+    kept.wait()
+    lead[HALF:] = block(0 * chip, 1)
+    mirror_begin(turned - 1, 0)
+    each(0, 1, compute(1))
+    for d in range(SIDE - 1):
+        lead_copy(d).start()
+    each(1, turned + 1, compute(1))
+    each(turned, total, lambda index: z_forward(index, 0))
+    each(turned + 1, total, compute(1))
     leading = front_ref[...] + weight_ref[0] * lead[:, :LEAD]
     for d in range(SIDE - 1):
         lead_copy(d).wait()
         leading = leading + weight_ref[d + 1] * lead_landing[d]
     upper_own[...] = leading
-    z_forward(0)
+    z_forward(0, 1)
     steps[0]()
-    z_forward(1)
+    z_forward(1, 1)
     steps[1]()
     steps[2]()
-    z_forward(2)
+    z_forward(2, 1)
     steps[3]()
+    z_begin(turned, 1)
+    z_forward(3, 1)
     steps[4]()
-    z_forward(3)
     steps[5]()
+    z_forward(4, 1)
+    z_begin(turned + 1, 1)
     steps[6]()
-    z_forward(4)
-    steps[7]()
-    z_forward(5)
-
-    def z_rest(index, carry):
-        z_begin(index)
-        return carry
-
-    lax.fori_loop(turned, total, z_rest, 0)
-    for step in steps[8:]:
+    z_forward(5, 1)
+    each(turned + 2, total, lambda index: z_begin(index, 1))
+    for step in steps[7:]:
         step()
-    lax.fori_loop(0, turned, fold, 0)
-
-    def forward(index, carry):
-        z_forward(index)
-        return carry
-
-    lax.fori_loop(turned, turned + 1, forward, 0)
-    for k in range(2):
-        mirror_copy(turned - 1, k).start()
-    lax.fori_loop(turned + 1, total, forward, 0)
-
-    def own_sum(index, carry):
-        z_sum(index)
-        return carry
-
-    lax.fori_loop(turned, total, own_sum, 0)
-
-    def drain(index, carry):
-        for which in range(4):
-            z_copy(index, which).wait_send()
-        return carry
-
-    lax.fori_loop(0, total, drain, 0)
-
-    def settle(index, carry):
-        for k in range(2):
-            mirror_copy(index, k).wait_send()
-            mirror_copy(index, k, True).wait_recv()
-        return carry
-
-    lax.fori_loop(0, turned, settle, 0)
-
-
-def post(weights, places, columns, inverse, moved, front):
+    each(0, turned, fold(1))
+    each(turned, turned + 2, lambda index: z_forward(index, 1))
+    mirror_begin(turned - 1, 1)
+    factor_into(pivots_ref[0], all_ref[:PMAX, :], upper_inverse_ref, work)
+    each(turned + 2, total, lambda index: z_forward(index, 1))
+    each(turned, total, lambda index: z_sum(index, 0))
+    each(turned, total, lambda index: z_sum(index, 1))
+
+    def drain(index):
+        for half in range(2):
+            for which in range(4):
+                z_copy(index, half, which).wait_send()
+
+    def settle(index):
+        for half in range(2):
+            for k in range(2):
+                mirror_copy(index, half, k).wait_send()
+                mirror_copy(index, half, k, True).wait_recv()
+
+    each(0, total, drain)
+    each(0, turned, settle)
+
+
+def post(weights, pivots, places, columns, inverse, moved, later, front):
     turned = len(TURNED)
     total = turned + len(SELF)
     dma = pltpu.SemaphoreType.DMA
     whole = lambda shape: pl.BlockSpec(shape, lambda i: (0,) * len(shape))
-    outs = [(ROWS, PMAX), (ORDER, PMAX), (total, ROWS, WIDE), (turned, 2, ROWS, ROWS)]
+    outs = [(ROWS, PMAX), (ORDER, PMAX), (PMAX, PMAX), (total, ROWS, WIDE), (turned, 2, 2, ROWS, HALF)]
     return pl.pallas_call(
         post_kernel,
         grid=(1,),
         out_shape=tuple(jax.ShapeDtypeStruct(shape, F32) for shape in outs),
         in_specs=[
             pl.BlockSpec(memory_space=pltpu.SMEM),
+            pl.BlockSpec(memory_space=pltpu.SMEM),
             whole(places.shape),
             whole((ORDER, PMAX)),
             whole((PMAX, PMAX)),
-            whole((CHIPS, ROWS, WIDE)),
+            whole((CHIPS, HALF, WIDE)),
+            whole((CHIPS, HALF, WIDE)),
             pl.BlockSpec((ROWS, LEAD), lambda i: (0, 0)),
         ],
         out_specs=tuple(whole(shape) for shape in outs),
         scratch_shapes=[
+            pltpu.VMEM((CHIPS, HALF, WIDE), F32),
             pltpu.VMEM((total, ROWS, WIDE), F32),
             pltpu.VMEM((ROWS, WIDE), F32),
             pltpu.VMEM((SIDE - 1, ROWS, LEAD), F32),
             pltpu.VMEM((ROWS, LEAD), F32),
             pltpu.VMEM((SIDE - 1, total, ROWS, WIDE), F32),
-            pltpu.VMEM((turned, 2, ROWS, ROWS), F32),
-            pltpu.VMEM((ROWS, 2 * WIDE), F32),
+            pltpu.VMEM((turned, 2, 2, ROWS, HALF), F32),
+            pltpu.VMEM((HALF, 2 * WIDE), F32),
             pltpu.VMEM((ROWS, PMAX), F32),
+            pltpu.VMEM((PMAX, 2 * PMAX), F32),
             dma,
             dma((36,)),
             dma((36,)),
-            dma((4 * total,)),
-            dma((4 * total,)),
-            dma((2 * turned,)),
-            dma((2 * turned,)),
+            dma((8 * total,)),
+            dma((8 * total,)),
+            dma((4 * turned,)),
+            dma((4 * turned,)),
             dma((SIDE - 1,)),
             dma((SIDE - 1,)),
+            dma((CHIPS - 1,)),
+            dma((CHIPS - 1,)),
+            dma,
         ],
         compiler_params=pltpu.CompilerParams(collective_id=1, has_side_effects=True),
         cost_estimate=pl.CostEstimate(flops=400_000_000, bytes_accessed=25_000_000, transcendentals=0),
         name="post",
-    )(weights, places, columns, inverse, moved, front)
+    )(weights, pivots, places, columns, inverse, moved, later, front)
 
 
 def parent_kernel(
@@ -572,7 +631,7 @@
 
     @pl.when(step >= sums)
     def _():
-        mirror = jnp.concatenate([mirror_ref[0, 0], mirror_ref[0, 1]], axis=1)
+        mirror = jnp.concatenate([mirror_ref[0, k, half] for k in range(2) for half in range(2)], axis=1)
         schur_ref[...] = jnp.where(keep, total + mirror, 0.0)
 
 
@@ -587,7 +646,7 @@
             pl.BlockSpec((WIDE, PMAX), lambda i, order: (order[i], 0)),
             pl.BlockSpec((PMAX, PMAX), lambda i, order: (0, 0)),
             pl.BlockSpec((1, ROWS, WIDE), lambda i, order: (jnp.minimum(i, count - 1), 0, 0)),
-            pl.BlockSpec((1, 2, ROWS, ROWS), lambda i, order: (jnp.maximum(i - count, 0), 0, 0, 0)),
+            pl.BlockSpec((1, 2, 2, ROWS, HALF), lambda i, order: (jnp.maximum(i - count, 0), 0, 0, 0, 0)),
             pl.BlockSpec((ROWS, WIDE), lambda i, order: (0, order[i])),
         ],
         out_specs=(
@@ -624,12 +683,13 @@
     line = jnp.where(position >= pivots, child_maps[front_group], -1)
     line = jnp.pad(line, (0, 2 * WIDE), constant_values=-1)
     places = jnp.broadcast_to(line[None], (8, line.shape[0]))
-    columns, turned = front(front_rows, places)
+    columns, turned, later = front(front_rows, places)
     same_core = [[2 * c + k for c in range(CHIPS)] for k in range(2)]
     moved = lax.all_to_all(turned, "grid", 0, 0, axis_index_groups=same_core)
     inverse = inverse_factor(pivots, columns)
-    panel_rows, upper_columns, sums, mirror = post(weights, places, columns, inverse, moved, parent_fronts[0])
-    upper_inverse = inverse_factor(upper_pivots, upper_columns)
+    panel_rows, upper_columns, upper_inverse, sums, mirror = post(
+        weights, upper_pivots, places, columns, inverse, moved, later, parent_fronts[0]
+    )
     upper_panel, upper_schur = parent_schur(
         order, upper_pivots, upper_columns, upper_inverse, sums, mirror, parent_fronts[0]
     )

time: 276 us -> 231 us (0.84)
  waiting for transfers between devices: 47.1 us -> 14 us
  Pallas kernels: 215 us -> 203 us
    all_to_all x1, waiting for transfers between devices: 47.1 us -> 14 us  [on_device(): moved = lax.all_to_all(turned, 'grid', 0, 0, axis_index_groups=same_core)]
    pallas_call x2 -> x1, Pallas kernels: 30.3 us -> 17.1 us  [inverse_factor(): pl.pallas_call(cholesky_kernel, grid=(1,), out_shape=jax.ShapeDtypeStruct...]
  transfers between devices with their start and end apart: 1 -> 1, of which waited for: 1 -> 1; matrix products, arithmetic and copies ran while one was open for 1% -> 1% of each run, Pallas kernels for 6% -> 7%
where the time goes in v5:
time: 231 us; the launch traced here: 230 us
  Pallas kernels  203 us (88%)
  waiting for transfers between devices  14 us (6%)
  starting transfers between devices  5.6 us (2%)
  local copies, waits for them, and re-layouts  5.33 us (2%)
    pallas_call x1, Pallas kernels, post(): pl.pallas_call(post_kernel, grid=(1,), out_shape=tuple((jax.ShapeDtypeStr...  135 us
    pallas_call x1, Pallas kernels, front(): pl.pallas_call(front_kernel, grid=(1,), out_shape=(jax.ShapeDtypeStruct((...  31.5 us
    pallas_call x1, Pallas kernels, parent_schur(): pl.pallas_call(parent_kernel, grid_spec=spec, out_shape=(jax.ShapeDtypeSt...  18.9 us
    pallas_call x1, Pallas kernels, inverse_factor(): pl.pallas_call(cholesky_kernel, grid=(1,), out_shape=jax.ShapeDtypeStruct...  17.1 us
    all_to_all x1, waiting for transfers between devices, on_device(): moved = lax.all_to_all(turned, 'grid', 0, 0, axis_index_groups=same_core)  14 us
    all_to_all x1, starting transfers between devices, on_device(): moved = lax.all_to_all(turned, 'grid', 0, 0, axis_index_groups=same_core)  5.6 us
  transfers between devices with their start and end apart: 1, of which 1 were waited for; matrix products, arithmetic and copies ran while one was open for 1% of the time, Pallas kernels for 7%

profile of v5, /device:TPU:0, one launch (start us, length us, event | category | flops | bytes accessed | tf_op | source)
XLA Modules:
  0.0 230.5 jit_solution(3675602846934333261)
XLA Ops:
  0.6 0.0 copy-start
  0.7 1.3 dynamic_slice.10.pivots_ref
  1.9 0.0 copy-done
  2.0 0.7 fusion
  2.6 0.7 broadcast_in_dim.75.places_ref
  3.3 31.5 %front.1 = (f32[6144,256]{1,0:T(8,128)}, f32[16,96,384]{2,1,0:T(8,128)}, f32[16,96,384]{2,1,0:T(8,128)}) custom-call(s32[8,6912]{1,0:T(8,128)} %broadcast_in_dim.75.places_ref, f32[192,6144]{1,0:T(8,128)} %bitcast.9, f32[192,6144]{1,0:T(8,128)} %bitcast.10), custom_call_target="tpu_custom_call" | custom-call | flops 400000000 | bytes 25000000 | tf_op jit(solution)/shard_map/front/pallas_call | solution.py:291
  34.8 0.0 copy-start.4
  34.8 0.0 copy-start.1
  34.8 5.6 %all-to-all-start = ((f32[16,96,384]{2,1,0:T(8,128)}), f32[16,96,384]{2,1,0:T(8,128)S(1)}, u32[]{:S(2)}, u32[]{:S(2)}) async-start(f32[16,96,384]{2,1,0:T(8,128)} %get-tuple-element.14), calls=%async_computation | async-start | bytes 4718592 | tf_op jit(solution)/shard_map/all_to_all | solution.py:688
  40.5 0.0 copy-done.4
  40.5 0.6 dynamic_slice.9.pivots_ref
  41.1 0.0 copy-done.1
  41.1 0.6 gather_fusion
  41.8 17.1 %inverse_factor.1.inverse_ref = f32[256,256]{1,0:T(8,128)} custom-call(s32[1]{0:T(128)} %dynamic_slice.10.pivots_ref, f32[6144,256]{1,0:T(8,128)} %get-tuple-element.13.block_ref.columns_ref), custom_call_target="tpu_custom_call" | custom-call | flops 400000000 | bytes 524288 | tf_op jit(solution)/shard_map/inverse_factor/pallas_call | solution.py:127
  58.9 0.6 compare_select_fusion.15.order_ref
  59.5 0.5 compare_convert_fusion.weight_ref
  60.0 14.0 %all-to-all-done.moved_ref = f32[16,96,384]{2,1,0:T(8,128)S(1)} async-done(((f32[16,96,384]{2,1,0:T(8,128)}), f32[16,96,384]{2,1,0:T(8,128)S(1)}, u32[]{:S(2)}, u32[]{:S(2)}) %all-to-all-start) | async-done | bytes 2359328 | tf_op jit(solution)/shard_map/all_to_all | solution.py:688
  74.0 0.0 copy-start.2
  74.0 1.4 copy-done.2
  75.4 135.5 %post.1 = (f32[192,256]{1,0:T(8,128)}, f32[6144,256]{1,0:T(8,128)}, f32[256,256]{1,0:T(8,128)}, f32[10,192,384]{2,1,0:T(8,128)}, f32[6,2,2,192,96]{4,3,2,1,0:T(8,128)}) custom-call(f32[4]{0:T(128)} %compare_convert_fusion.weight_ref, s32[1]{0:T(128)} %dynamic_slice.9.pivots_ref, s32[8,6912]{1,0:T(8,128)} %broadcast_in_dim.75.places_ref, ...), custom_call_target="tpu_custom_call" | custom-call | flops 400000000 | bytes 25000000 | tf_op jit(solution)/shard_map/post/pallas_call | solution.py:563
  210.9 0.0 copy-start.3
  210.9 18.9 %parent_schur.1 = (f32[192,256]{1,0:T(8,128)}, f32[192,6144]{1,0:T(8,128)}) custom-call(s32[17]{0:T(128)} %compare_select_fusion.15.order_ref, s32[1]{0:T(128)} %dynamic_slice.9.pivots_ref, f32[6144,256]{1,0:T(8,128)} %get-tuple-element.17.own_ref.here_ref, f32[6144,256]{1,0:T(8,128)} %get-tuple-element.17.own_ref.here_ref, ...), custom_call_target="tpu_custom_call" | custom-call | flops 400000000 | bytes 30000000 | tf_op jit(solution)/shard_map/parent_schur/pallas_call | solution.py:658
  229.8 0.0 copy-done.3
  229.8 0.7 copy.10
  (4 shorter events, 0.0 us)
Async XLA Ops:
  0.6 1.3 copy-start
  34.8 5.7 %copy-start.4 = (s32[4]{0:T(128)S(1)}, s32[4]{0:T(128)}, u32[]{:S(2)}) copy-start(s32[4]{0:T(128)} %param.11) | copy-start | bytes 52
  34.8 6.3 %copy-start.1 = (s32[4]{0:T(128)S(1)}, s32[4]{0:T(128)}, u32[]{:S(2)}) copy-start(s32[4]{0:T(128)} %param.9) | copy-start | bytes 52
  34.8 39.1 %all-to-all-start = ((f32[16,96,384]{2,1,0:T(8,128)}), f32[16,96,384]{2,1,0:T(8,128)S(1)}, u32[]{:S(2)}, u32[]{:S(2)}) async-start(f32[16,96,384]{2,1,0:T(8,128)} %get-tuple-element.14), calls=%async_computation | async-start | bytes 4718592 | tf_op jit(solution)/shard_map/all_to_all | solution.py:688
  74.0 1.4 copy-start.2
  210.9 18.9 %copy-start.3 = (f32[192,256]{1,0:T(8,128)S(1)}, f32[192,256]{1,0:T(8,128)}, u32[]{:S(2)}) copy-start(f32[192,256]{1,0:T(8,128)} %get-tuple-element.16) | copy-start | bytes 589828
